TPU v7x, 512 devices: a whole 4x8x8 slice. The times are simulated.
512 devices in a mesh: orb: 4 (over x), gx: 8 (over y), gyz: 16 (over z, core).
Axes of the slice: x: 4, y: 8, z: 8, core: 2. Of those that a mesh axis runs over, the one named last changes fastest.
Arguments:
- orbitals: float32 [2, 12, 128, 128, 128], P(None, 'orb', 'gx', 'gyz'), parts along dimension 1, may hold values from -12 to 12
- potential: float32 [128, 128, 128], P('gx', 'gyz'), may hold values from -8 to 60
Outputs:
- evolved: float32 [2, 12, 128, 128, 128], P(None, 'orb', 'gx', 'gyz'), parts along dimension 1
- residual: float32 [2, 12, 128, 128, 128], P(None, 'orb', 'gx', 'gyz'), parts along dimension 1
There are 4 independent parts, one for each index of `orb`. A program takes and returns all parts, laid end to end along the dimension named above; an argument that names none is the same for every part. Nothing has to cross between parts.
All inputs are finite; a program needn't handle non-finite values.
Results may differ from a plain program's by a relative error of at most 0.0003.
Values sent between devices are 32-bit elements; how exact they have to be, the bound alone decides.
A program may use at most 64 MiB of HBM per device.

v0:
```python
import jax
import jax.numpy as jnp
from jax import lax
from jax.sharding import Mesh
from jax.sharding import PartitionSpec as P

ITERS = 4
GX_GYZ = ("gx", "gyz_0", "gyz_1")
GYZ = ("gyz_0", "gyz_1")


SPACING = 0.25
HALF_STEP = 0.05
COEFF_NEAR = 4.0 / 3.0
COEFF_FAR = -1.0 / 12.0
COEFF_SELF = -2.5


def padded_2(array, sides, width):
    edges = {}
    for axis, dim in sides:
        size, length = (lax.axis_size(axis), array.shape[dim])
        up = [(i, (i + 1) % size) for i in range(size - 1)]
        last = lax.slice_in_dim(array, length - width, length, axis=dim)
        leading = lax.slice_in_dim(array, 0, width, axis=dim)
        edges[dim] = (
            lax.ppermute(last, axis, up),
            lax.ppermute(leading, axis, [(b, a) for a, b in up]),
        )
    done = []
    for _, dim in sides:
        low, high = edges[dim]
        around = [(width, width) if d in done else (0, 0) for d in range(array.ndim)]
        array = jnp.concatenate([jnp.pad(low, around), array, jnp.pad(high, around)], axis=dim)
        done.append(dim)
    return array


def by_axis(array, axes):
    for axis in axes:
        array = lax.psum(array, axis)
    return array


def laplace_apply(padded, potential):
    extent = (padded.shape[2] - 4, padded.shape[3] - 4, padded.shape[4] - 4)

    def window(shift_x, shift_y, shift_z):
        return padded[
            :,
            :,
            2 + shift_x : 2 + shift_x + extent[0],
            2 + shift_y : 2 + shift_y + extent[1],
            2 + shift_z : 2 + shift_z + extent[2],
        ]

    center = window(0, 0, 0)
    summed = 3.0 * COEFF_SELF * center
    for offset, weight in ((1, COEFF_NEAR), (2, COEFF_FAR)):
        summed = summed + weight * (
            window(offset, 0, 0)
            + window(-offset, 0, 0)
            + window(0, offset, 0)
            + window(0, -offset, 0)
            + window(0, 0, offset)
            + window(0, 0, -offset)
        )
    return -0.5 / SPACING**2 * summed + potential * center


def pad_depth(vector):
    return jnp.pad(vector, ((0, 0), (0, 0), (0, 0), (0, 0), (2, 2)))


def system(vector, applied):
    return jnp.stack([vector[0] - HALF_STEP * applied[1], vector[1] + HALF_STEP * applied[0]])


def precondition(vector, potential):
    diagonal = HALF_STEP * (3.75 / SPACING**2 + potential)
    divisor = 1.0 + diagonal * diagonal
    return jnp.stack(
        [(vector[0] + diagonal * vector[1]) / divisor, (vector[1] - diagonal * vector[0]) / divisor]
    )


def braket(left, right):
    real_part = jnp.sum(left[0] * right[0] + left[1] * right[1], axis=(1, 2, 3))
    imag_part = jnp.sum(left[0] * right[1] - left[1] * right[0], axis=(1, 2, 3))
    return (real_part, imag_part)


def times_complex(first, second):
    return (
        first[0] * second[0] - first[1] * second[1],
        first[0] * second[1] + first[1] * second[0],
    )


def divide_complex(first, second):
    modulus = second[0] * second[0] + second[1] * second[1]
    return (
        (first[0] * second[0] + first[1] * second[1]) / modulus,
        (first[1] * second[0] - first[0] * second[1]) / modulus,
    )


def scale_complex(coeff, vector):
    real_coef = coeff[0][:, None, None, None]
    imag_coef = coeff[1][:, None, None, None]
    return jnp.stack(
        [
            real_coef * vector[0] - imag_coef * vector[1],
            real_coef * vector[1] + imag_coef * vector[0],
        ]
    )


def shards(orbitals, potential):

    def apply_shallow(vector):
        padded = padded_2(vector, (("gx", 2), (GYZ, 3)), 2)
        return laplace_apply(pad_depth(padded), potential)

    h_orbitals = apply_shallow(orbitals)
    residual = jnp.stack([2.0 * HALF_STEP * h_orbitals[1], -2.0 * HALF_STEP * h_orbitals[0]])
    evolved = orbitals
    shadow = residual
    direction = residual
    rho_now = jax.tree.map(lambda part: by_axis(part, GX_GYZ), braket(shadow, residual))
    for iteration in range(ITERS):
        dir_hat = precondition(direction, potential)
        image = system(dir_hat, apply_shallow(dir_hat))
        alpha_step = divide_complex(
            rho_now, jax.tree.map(lambda part: by_axis(part, GX_GYZ), braket(shadow, image))
        )
        half_step = residual - scale_complex(alpha_step, image)
        half_hat = precondition(half_step, potential)
        second = system(half_hat, apply_shallow(half_hat))
        cross_local = braket(second, half_step)
        norm_local = jnp.sum(second * second, axis=(0, 2, 3, 4))
        shadow_half = braket(shadow, half_step)
        shadow_second = braket(shadow, second)
        summed = (
            by_axis(cross_local[0], GX_GYZ),
            by_axis(cross_local[1], GX_GYZ),
            by_axis(norm_local, GX_GYZ),
            by_axis(shadow_half[0], GX_GYZ),
            by_axis(shadow_half[1], GX_GYZ),
            by_axis(shadow_second[0], GX_GYZ),
            by_axis(shadow_second[1], GX_GYZ),
        )
        cross_real, cross_imag, norm_second = (summed[0], summed[1], summed[2])
        omega_step = (cross_real / norm_second, cross_imag / norm_second)
        evolved = evolved + scale_complex(alpha_step, dir_hat) + scale_complex(omega_step, half_hat)
        residual = half_step - scale_complex(omega_step, second)
        if iteration + 1 < ITERS:
            along_second = times_complex(omega_step, (summed[5], summed[6]))
            rho_next = (summed[3] - along_second[0], summed[4] - along_second[1])
            beta_step = times_complex(
                divide_complex(rho_next, rho_now), divide_complex(alpha_step, omega_step)
            )
            direction = residual + scale_complex(
                beta_step, direction - scale_complex(omega_step, image)
            )
            rho_now = rho_next
    return (evolved, residual)


def solution(mesh):
    finer = Mesh(
        mesh.devices.reshape(mesh.shape["orb"], mesh.shape["gx"], 8, 2),
        ("orb", "gx", "gyz_0", "gyz_1"),
    )
    return jax.shard_map(
        shards,
        mesh=finer,
        in_specs=(P(None, "orb", "gx", GYZ, None), P("gx", GYZ, None)),
        out_specs=(P(None, "orb", "gx", GYZ, None), P(None, "orb", "gx", GYZ, None)),
        check_vma=False,
    )
```

profile of v0, /device:TPU:6, one launch (start us, length us, event | category | flops | bytes accessed | tf_op | source)
XLA Modules:
  0.0 459.1 jit_solution(8637743133134373983)
XLA Ops:
  2.8 4.5 collective-permute-start.1
  13.2 2.4 collective-permute-done.2
  17.5 3.5 collective-permute-start.5
  22.4 4.9 %collective-permute-start.7 = (f32[2,3,16,2,128]{4,3,2,1,0:T(2,128)S(1)}, f32[2,3,16,2,128]{4,3,2,1,0:T(2,128)S(1)}, u32[]{:S(2)}, u32[]{:S(2)}) collective-permute-start(f32[2,3,16,2,128]{4,3,2,1,0:T(2,128)S(1)} %get-tuple-element.304), channel_id=1, source_target_pairs={{0,1},{1,2},{2,3},{3,4},{4,5},{5,6},{6,7},{7,8},{8,9},{9,10},{10,1... | collective-permute-start | bytes 294920 | tf_op jit(solution)/shard_map/ppermute | solution.py:27
  28.7 1.7 collective-permute-done.6
  32.6 18.0 %all-reduce.42 = (f32[3]{0:T(128)S(1)}, f32[3]{0:T(128)S(1)}, f32[3]{0:T(128)S(1)}, f32[3]{0:T(128)S(1)}) all-reduce(f32[3]{0:T(128)S(1)} %get-tuple-element.43, f32[3]{0:T(128)S(1)} %get-tuple-element.3, f32[3]{0:T(128)S(1)} %get-tuple-element.42, f32[3]{0:T(128)S(1)} %get-tuple-element.2), channel_id=1, replica_groups=mesh['orb'=4,'gx'=8,'gyz_0'=8,'gyz_1'=2] {'gx'}, use_global_device_ids=true, to_apply=%region_1.2 | all-reduce | flops 12 | bytes 96 | tf_op jit(solution)/shard_map/psum | solution.py:41
  50.6 23.7 %all-reduce.34 = (f32[3]{0:T(128)S(1)}, f32[3]{0:T(128)S(1)}, f32[3]{0:T(128)S(1)}, f32[3]{0:T(128)S(1)}) all-reduce(f32[3]{0:T(128)S(1)} %get-tuple-element.108, f32[3]{0:T(128)S(1)} %get-tuple-element.109, f32[3]{0:T(128)S(1)} %get-tuple-element.110, ...), channel_id=1, replica_groups=mesh['orb'=4,'gx'=8,'gyz_0'=8,'gyz_1'=2] {'gyz_0'}, use_global_device_ids=true, to_apply=%region_2.3 | all-reduce | flops 12 | bytes 96 | tf_op jit(solution)/shard_map/psum | solution.py:41
  74.2 2.5 all-reduce.50
  77.8 3.3 collective-permute-start.9
  82.4 1.8 collective-permute-start.11
  89.9 17.7 %all-reduce.41 = (f32[3]{0:T(128)S(1)}, f32[3]{0:T(128)S(1)}, f32[3]{0:T(128)S(1)}, f32[3]{0:T(128)S(1)}, f32[3]{0:T(128)S(1)}, /*index=5*/f32[3]{0:T(128)S(1)}, f32[3]{0:T(128)S(1)}) all-reduce(f32[3]{0:T(128)S(1)} %get-tuple-element.40, f32[3]{0:T(128)S(1)} %fusion.80, ...), channel_id=1, replica_groups=mesh['orb'=4,'gx'=8,'gyz_0'=8,'gyz_1'=2] {'gx'}, use_global_device_ids=true, to_apply=%region_25.26 | all-reduce | flops 21 | bytes 168 | tf_op jit(solution)/shard_map/psum | solution.py:41
  107.6 18.1 %all-reduce.33 = (f32[3]{0:T(128)S(1)}, f32[3]{0:T(128)S(1)}, f32[3]{0:T(128)S(1)}, f32[3]{0:T(128)S(1)}, f32[3]{0:T(128)S(1)}, /*index=5*/f32[3]{0:T(128)S(1)}, f32[3]{0:T(128)S(1)}) all-reduce(f32[3]{0:T(128)S(1)} %get-tuple-element.101, ...), channel_id=1, replica_groups=mesh['orb'=4,'gx'=8,'gyz_0'=8,'gyz_1'=2] {'gyz_0'}, use_global_device_ids=true, to_apply=%region_26.27 | all-reduce | flops 21 | bytes 168 | tf_op jit(solution)/shard_map/psum | solution.py:41
  125.6 2.5 all-reduce.49
  129.5 2.3 collective-permute-start.13
  133.2 1.8 collective-permute-start.15
  140.3 17.7 %all-reduce.40 = (f32[3]{0:T(128)S(1)}, f32[3]{0:T(128)S(1)}) all-reduce(f32[3]{0:T(128)S(1)} %get-tuple-element.23, f32[3]{0:T(128)S(1)} %get-tuple-element.22), channel_id=1, replica_groups=mesh['orb'=4,'gx'=8,'gyz_0'=8,'gyz_1'=2] {'gx'}, use_global_device_ids=true, to_apply=%region_49.50 | all-reduce | flops 6 | bytes 48 | tf_op jit(solution)/shard_map/psum | solution.py:41
  158.0 18.6 %all-reduce.32 = (f32[3]{0:T(128)S(1)}, f32[3]{0:T(128)S(1)}) all-reduce(f32[3]{0:T(128)S(1)} %get-tuple-element.99, f32[3]{0:T(128)S(1)} %get-tuple-element.100), channel_id=1, replica_groups=mesh['orb'=4,'gx'=8,'gyz_0'=8,'gyz_1'=2] {'gyz_0'}, use_global_device_ids=true, to_apply=%region_50.51 | all-reduce | flops 6 | bytes 48 | tf_op jit(solution)/shard_map/psum | solution.py:41
  176.6 2.5 all-reduce.48
  180.7 2.2 collective-permute-start.17
  184.3 1.8 collective-permute-start.19
  192.8 18.1 %all-reduce.39 = (f32[3]{0:T(128)S(1)}, f32[3]{0:T(128)S(1)}, f32[3]{0:T(128)S(1)}, f32[3]{0:T(128)S(1)}, f32[3]{0:T(128)S(1)}, /*index=5*/f32[3]{0:T(128)S(1)}, f32[3]{0:T(128)S(1)}) all-reduce(f32[3]{0:T(128)} %get-tuple-element.36, f32[3]{0:T(128)S(1)} %fusion.81, ...), channel_id=1, replica_groups=mesh['orb'=4,'gx'=8,'gyz_0'=8,'gyz_1'=2] {'gx'}, use_global_device_ids=true, to_apply=%region_61.62 | all-reduce | flops 21 | bytes 168 | tf_op jit(solution)/shard_map/psum | solution.py:41
  211.0 18.4 %all-reduce.31 = (f32[3]{0:T(128)S(1)}, f32[3]{0:T(128)S(1)}, f32[3]{0:T(128)S(1)}, f32[3]{0:T(128)S(1)}, f32[3]{0:T(128)S(1)}, /*index=5*/f32[3]{0:T(128)S(1)}, f32[3]{0:T(128)S(1)}) all-reduce(f32[3]{0:T(128)S(1)} %get-tuple-element.92, f32[3]{0:T(128)S(1)} %get-tuple-element.93, ...), channel_id=1, replica_groups=mesh['orb'=4,'gx'=8,'gyz_0'=8,'gyz_1'=2] {'gyz_0'}, use_global_device_ids=true, to_apply=%region_62.63 | all-reduce | flops 21 | bytes 168 | tf_op jit(solution)/shard_map/psum | solution.py:41
  229.4 2.5 all-reduce.47
  232.5 2.1 multiply_subtract_fusion.12
  236.6 2.3 collective-permute-start.21
  240.3 1.8 collective-permute-start.23
  248.1 17.8 %all-reduce.38 = (f32[3]{0:T(128)S(1)}, f32[3]{0:T(128)S(1)}) all-reduce(f32[3]{0:T(128)S(1)} %get-tuple-element.15, f32[3]{0:T(128)S(1)} %get-tuple-element.14), channel_id=1, replica_groups=mesh['orb'=4,'gx'=8,'gyz_0'=8,'gyz_1'=2] {'gx'}, use_global_device_ids=true, to_apply=%region_85.86 | all-reduce | flops 6 | bytes 48 | tf_op jit(solution)/shard_map/psum | solution.py:41
  265.9 18.4 %all-reduce.30 = (f32[3]{0:T(128)S(1)}, f32[3]{0:T(128)S(1)}) all-reduce(f32[3]{0:T(128)S(1)} %get-tuple-element.90, f32[3]{0:T(128)S(1)} %get-tuple-element.91), channel_id=1, replica_groups=mesh['orb'=4,'gx'=8,'gyz_0'=8,'gyz_1'=2] {'gyz_0'}, use_global_device_ids=true, to_apply=%region_86.87 | all-reduce | flops 6 | bytes 48 | tf_op jit(solution)/shard_map/psum | solution.py:41
  284.3 2.5 all-reduce.46
  286.8 1.9 multiply_subtract_fusion.8
  289.6 2.3 collective-permute-start.25
  293.2 1.8 collective-permute-start.27
  302.3 18.7 %all-reduce.37 = (f32[3]{0:T(128)}, f32[3]{0:T(128)}, f32[3]{0:T(128)}, f32[3]{0:T(128)}, f32[3]{0:T(128)}, /*index=5*/f32[3]{0:T(128)}, f32[3]{0:T(128)}) all-reduce(f32[3]{0:T(128)} %get-tuple-element.32, f32[3]{0:T(128)} %fusion.82, f32[3]{0:T(128)} %get-tuple-element.33, ...), channel_id=1, replica_groups=mesh['orb'=4,'gx'=8,'gyz_0'=8,'gyz_1'=2] {'gx'}, use_global_device_ids=true, to_apply=%region_97.98 | all-reduce | flops 21 | bytes 168 | tf_op jit(solution)/shard_map/psum | solution.py:41
  321.0 19.1 %all-reduce.29 = (f32[3]{0:T(128)}, f32[3]{0:T(128)}, f32[3]{0:T(128)}, f32[3]{0:T(128)}, f32[3]{0:T(128)}, /*index=5*/f32[3]{0:T(128)}, f32[3]{0:T(128)}) all-reduce(f32[3]{0:T(128)} %get-tuple-element.83, f32[3]{0:T(128)} %get-tuple-element.84, ...), channel_id=1, replica_groups=mesh['orb'=4,'gx'=8,'gyz_0'=8,'gyz_1'=2] {'gyz_0'}, use_global_device_ids=true, to_apply=%region_98.99 | all-reduce | flops 21 | bytes 168 | tf_op jit(solution)/shard_map/psum | solution.py:41
  340.2 3.2 all-reduce.45
  344.7 2.2 multiply_subtract_fusion.6
  348.2 2.3 collective-permute-start.29
  351.9 1.8 collective-permute-start.31
  359.4 17.8 %all-reduce.36 = (f32[3]{0:T(128)S(1)}, f32[3]{0:T(128)S(1)}) all-reduce(f32[3]{0:T(128)S(1)} %get-tuple-element.7, f32[3]{0:T(128)S(1)} %get-tuple-element.6), channel_id=1, replica_groups=mesh['orb'=4,'gx'=8,'gyz_0'=8,'gyz_1'=2] {'gx'}, use_global_device_ids=true, to_apply=%region_121.122 | all-reduce | flops 6 | bytes 48 | tf_op jit(solution)/shard_map/psum | solution.py:41
  377.2 18.4 %all-reduce.28 = (f32[3]{0:T(128)S(1)}, f32[3]{0:T(128)S(1)}) all-reduce(f32[3]{0:T(128)S(1)} %get-tuple-element.81, f32[3]{0:T(128)S(1)} %get-tuple-element.82), channel_id=1, replica_groups=mesh['orb'=4,'gx'=8,'gyz_0'=8,'gyz_1'=2] {'gyz_0'}, use_global_device_ids=true, to_apply=%region_122.123 | all-reduce | flops 6 | bytes 48 | tf_op jit(solution)/shard_map/psum | solution.py:41
  395.7 2.5 all-reduce.44
  398.1 2.0 multiply_subtract_fusion.2
  402.2 2.2 collective-permute-start.33
  405.8 1.8 collective-permute-start.35
  414.2 18.5 %all-reduce.35 = (f32[3]{0:T(128)S(1)}, f32[3]{0:T(128)}, f32[3]{0:T(128)}) all-reduce(f32[3]{0:T(128)S(1)} %get-tuple-element.5, f32[3]{0:T(128)S(1)} %fusion.83, f32[3]{0:T(128)S(1)} %get-tuple-element.4), channel_id=1, replica_groups=mesh['orb'=4,'gx'=8,'gyz_0'=8,'gyz_1'=2] {'gx'}, use_global_device_ids=true, to_apply=%region_133.134 | all-reduce | flops 9 | bytes 72 | tf_op jit(solution)/shard_map/psum | solution.py:41
  432.7 19.1 %all-reduce.27 = (f32[3]{0:T(128)}, f32[3]{0:T(128)}, f32[3]{0:T(128)}) all-reduce(f32[3]{0:T(128)S(1)} %get-tuple-element.78, f32[3]{0:T(128)} %get-tuple-element.79, f32[3]{0:T(128)} %get-tuple-element.80), channel_id=1, replica_groups=mesh['orb'=4,'gx'=8,'gyz_0'=8,'gyz_1'=2] {'gyz_0'}, use_global_device_ids=true, to_apply=%region_134.135 | all-reduce | flops 9 | bytes 72 | tf_op jit(solution)/shard_map/psum | solution.py:41
  451.9 2.6 all-reduce.43
  455.8 2.1 maximum_subtract_fusion.10
  (273 shorter events, 81.4 us)
Async XLA Ops:
  1.5 11.7 %collective-permute-start = (f32[2,3,2,8,128]{4,3,2,1,0:T(8,128)S(1)}, f32[2,3,2,8,128]{4,3,2,1,0:T(8,128)S(1)}, u32[]{:S(2)}, u32[]{:S(2)}) collective-permute-start(f32[2,3,2,8,128]{4,3,2,1,0:T(8,128)S(1)} %get-tuple-element.311), channel_id=1, source_target_pairs={{16,0},{32,16},{48,32},{64,48},{80,64},{96,80},{112,96},{17,1},{33... | collective-permute-start | bytes 147464 | tf_op jit(solution)/shard_map/ppermute | solution.py:28
  2.8 9.3 %collective-permute-start.1 = (f32[2,3,2,8,128]{4,3,2,1,0:T(8,128)S(1)}, f32[2,3,2,8,128]{4,3,2,1,0:T(8,128)S(1)}, u32[]{:S(2)}, u32[]{:S(2)}) collective-permute-start(f32[2,3,2,8,128]{4,3,2,1,0:T(8,128)S(1)} %get-tuple-element.312), channel_id=1, source_target_pairs={{0,16},{16,32},{32,48},{48,64},{64,80},{80,96},{96,112},{1,17},{17... | collective-permute-start | bytes 147464 | tf_op jit(solution)/shard_map/ppermute | solution.py:27
  8.5 4.7 %collective-permute-start.3 = (f32[2,3,16,2,128]{4,3,2,1,0:T(2,128)S(1)}, f32[2,3,16,2,128]{4,3,2,1,0:T(2,128)S(1)}, u32[]{:S(2)}, u32[]{:S(2)}) collective-permute-start(f32[2,3,16,2,128]{4,3,2,1,0:T(2,128)S(1)} %get-tuple-element.309), channel_id=1, source_target_pairs={{0,1},{1,2},{2,3},{3,4},{4,5},{5,6},{6,7},{7,8},{8,9},{9,10},{10,1... | collective-permute-start | bytes 294920 | tf_op jit(solution)/shard_map/ppermute | solution.py:27
  9.8 5.8 %collective-permute-start.2 = (f32[2,3,16,2,128]{4,3,2,1,0:T(2,128)S(1)}, f32[2,3,16,2,128]{4,3,2,1,0:T(2,128)S(1)}, u32[]{:S(2)}, u32[]{:S(2)}) collective-permute-start(f32[2,3,16,2,128]{4,3,2,1,0:T(2,128)S(1)} %get-tuple-element.310), channel_id=1, source_target_pairs={{1,0},{2,1},{3,2},{4,3},{5,4},{6,5},{7,6},{8,7},{9,8},{10,9},{11,1... | collective-permute-start | bytes 294920 | tf_op jit(solution)/shard_map/ppermute | solution.py:28
  13.1 3.6 copy-start
  13.1 3.6 copy-start.1
  17.5 11.0 %collective-permute-start.5 = (f32[2,3,2,8,128]{4,3,2,1,0:T(8,128)S(1)}, f32[2,3,2,8,128]{4,3,2,1,0:T(8,128)S(1)}, u32[]{:S(2)}, u32[]{:S(2)}) collective-permute-start(f32[2,3,2,8,128]{4,3,2,1,0:T(8,128)S(1)} %get-tuple-element.302), channel_id=1, source_target_pairs={{0,16},{16,32},{32,48},{48,64},{64,80},{80,96},{96,112},{1,17},{17... | collective-permute-start | bytes 147464 | tf_op jit(solution)/shard_map/ppermute | solution.py:27
  21.0 7.6 %collective-permute-start.4 = (f32[2,3,2,8,128]{4,3,2,1,0:T(8,128)S(1)}, f32[2,3,2,8,128]{4,3,2,1,0:T(8,128)S(1)}, u32[]{:S(2)}, u32[]{:S(2)}) collective-permute-start(f32[2,3,2,8,128]{4,3,2,1,0:T(8,128)S(1)} %get-tuple-element.303), channel_id=1, source_target_pairs={{16,0},{32,16},{48,32},{64,48},{80,64},{96,80},{112,96},{17,1},{33... | collective-permute-start | bytes 147464 | tf_op jit(solution)/shard_map/ppermute | solution.py:28
  22.4 6.3 %collective-permute-start.7 = (f32[2,3,16,2,128]{4,3,2,1,0:T(2,128)S(1)}, f32[2,3,16,2,128]{4,3,2,1,0:T(2,128)S(1)}, u32[]{:S(2)}, u32[]{:S(2)}) collective-permute-start(f32[2,3,16,2,128]{4,3,2,1,0:T(2,128)S(1)} %get-tuple-element.304), channel_id=1, source_target_pairs={{0,1},{1,2},{2,3},{3,4},{4,5},{5,6},{6,7},{7,8},{8,9},{9,10},{10,1... | collective-permute-start | bytes 294920 | tf_op jit(solution)/shard_map/ppermute | solution.py:27
  27.3 3.2 collective-permute-start.6
  77.8 7.7 %collective-permute-start.9 = (f32[2,3,2,8,128]{4,3,2,1,0:T(8,128)S(1)}, f32[2,3,2,8,128]{4,3,2,1,0:T(8,128)S(1)}, u32[]{:S(2)}, u32[]{:S(2)}) collective-permute-start(f32[2,3,2,8,128]{4,3,2,1,0:T(8,128)S(1)} %get-tuple-element.294), channel_id=1, source_target_pairs={{0,16},{16,32},{32,48},{48,64},{64,80},{80,96},{96,112},{1,17},{17... | collective-permute-start | bytes 147464 | tf_op jit(solution)/shard_map/ppermute | solution.py:27
  81.1 6.0 %collective-permute-start.8 = (f32[2,3,2,8,128]{4,3,2,1,0:T(8,128)S(1)}, f32[2,3,2,8,128]{4,3,2,1,0:T(8,128)S(1)}, u32[]{:S(2)}, u32[]{:S(2)}) collective-permute-start(f32[2,3,2,8,128]{4,3,2,1,0:T(8,128)S(1)} %get-tuple-element.295), channel_id=1, source_target_pairs={{16,0},{32,16},{48,32},{64,48},{80,64},{96,80},{112,96},{17,1},{33... | collective-permute-start | bytes 147464 | tf_op jit(solution)/shard_map/ppermute | solution.py:28
  82.4 4.7 %collective-permute-start.11 = (f32[2,3,16,2,128]{4,3,2,1,0:T(2,128)S(1)}, f32[2,3,16,2,128]{4,3,2,1,0:T(2,128)S(1)}, u32[]{:S(2)}, u32[]{:S(2)}) collective-permute-start(f32[2,3,16,2,128]{4,3,2,1,0:T(2,128)S(1)} %get-tuple-element.296), channel_id=1, source_target_pairs={{0,1},{1,2},{2,3},{3,4},{4,5},{5,6},{6,7},{7,8},{8,9},{9,10},{10,1... | collective-permute-start | bytes 294920 | tf_op jit(solution)/shard_map/ppermute | solution.py:27
  84.3 3.2 collective-permute-start.10
  128.1 50.9 %copy-start.42 = (f32[3]{0:T(128)}, f32[3]{0:T(128)S(1)}, u32[]{:S(2)}) copy-start(f32[3]{0:T(128)S(1)} %get-tuple-element.175) | copy-start | bytes 40
  128.1 50.9 %copy-start.43 = (f32[3]{0:T(128)}, f32[3]{0:T(128)S(1)}, u32[]{:S(2)}) copy-start(f32[3]{0:T(128)S(1)} %get-tuple-element.176) | copy-start | bytes 40
  129.3 3.9 copy-start.20
  129.3 3.9 copy-start.21
  129.5 6.8 %collective-permute-start.13 = (f32[2,3,2,8,128]{4,3,2,1,0:T(8,128)S(1)}, f32[2,3,2,8,128]{4,3,2,1,0:T(8,128)S(1)}, u32[]{:S(2)}, u32[]{:S(2)}) collective-permute-start(f32[2,3,2,8,128]{4,3,2,1,0:T(8,128)S(1)} %get-tuple-element.286), channel_id=1, source_target_pairs={{0,16},{16,32},{32,48},{48,64},{64,80},{80,96},{96,112},{1,17},{17... | collective-permute-start | bytes 147464 | tf_op jit(solution)/shard_map/ppermute | solution.py:27
  131.8 6.0 %collective-permute-start.12 = (f32[2,3,2,8,128]{4,3,2,1,0:T(8,128)S(1)}, f32[2,3,2,8,128]{4,3,2,1,0:T(8,128)S(1)}, u32[]{:S(2)}, u32[]{:S(2)}) collective-permute-start(f32[2,3,2,8,128]{4,3,2,1,0:T(8,128)S(1)} %get-tuple-element.287), channel_id=1, source_target_pairs={{16,0},{32,16},{48,32},{64,48},{80,64},{96,80},{112,96},{17,1},{33... | collective-permute-start | bytes 147464 | tf_op jit(solution)/shard_map/ppermute | solution.py:28
  133.2 4.7 %collective-permute-start.15 = (f32[2,3,16,2,128]{4,3,2,1,0:T(2,128)S(1)}, f32[2,3,16,2,128]{4,3,2,1,0:T(2,128)S(1)}, u32[]{:S(2)}, u32[]{:S(2)}) collective-permute-start(f32[2,3,16,2,128]{4,3,2,1,0:T(2,128)S(1)} %get-tuple-element.288), channel_id=1, source_target_pairs={{0,1},{1,2},{2,3},{3,4},{4,5},{5,6},{6,7},{7,8},{8,9},{9,10},{10,1... | collective-permute-start | bytes 294920 | tf_op jit(solution)/shard_map/ppermute | solution.py:27
  135.0 3.2 collective-permute-start.14
  180.7 6.7 %collective-permute-start.17 = (f32[2,3,2,8,128]{4,3,2,1,0:T(8,128)S(1)}, f32[2,3,2,8,128]{4,3,2,1,0:T(8,128)S(1)}, u32[]{:S(2)}, u32[]{:S(2)}) collective-permute-start(f32[2,3,2,8,128]{4,3,2,1,0:T(8,128)S(1)} %get-tuple-element.280), channel_id=1, source_target_pairs={{0,16},{16,32},{32,48},{48,64},{64,80},{80,96},{96,112},{1,17},{17... | collective-permute-start | bytes 147464 | tf_op jit(solution)/shard_map/ppermute | solution.py:27
  183.0 6.0 %collective-permute-start.16 = (f32[2,3,2,8,128]{4,3,2,1,0:T(8,128)S(1)}, f32[2,3,2,8,128]{4,3,2,1,0:T(8,128)S(1)}, u32[]{:S(2)}, u32[]{:S(2)}) collective-permute-start(f32[2,3,2,8,128]{4,3,2,1,0:T(8,128)S(1)} %get-tuple-element.281), channel_id=1, source_target_pairs={{16,0},{32,16},{48,32},{64,48},{80,64},{96,80},{112,96},{17,1},{33... | collective-permute-start | bytes 147464 | tf_op jit(solution)/shard_map/ppermute | solution.py:28
  184.3 4.7 %collective-permute-start.19 = (f32[2,3,16,2,128]{4,3,2,1,0:T(2,128)S(1)}, f32[2,3,16,2,128]{4,3,2,1,0:T(2,128)S(1)}, u32[]{:S(2)}, u32[]{:S(2)}) collective-permute-start(f32[2,3,16,2,128]{4,3,2,1,0:T(2,128)S(1)} %get-tuple-element.282), channel_id=1, source_target_pairs={{0,1},{1,2},{2,3},{3,4},{4,5},{5,6},{6,7},{7,8},{8,9},{9,10},{10,1... | collective-permute-start | bytes 294920 | tf_op jit(solution)/shard_map/ppermute | solution.py:27
  186.1 3.7 collective-permute-start.18
  236.6 6.8 %collective-permute-start.21 = (f32[2,3,2,8,128]{4,3,2,1,0:T(8,128)S(1)}, f32[2,3,2,8,128]{4,3,2,1,0:T(8,128)S(1)}, u32[]{:S(2)}, u32[]{:S(2)}) collective-permute-start(f32[2,3,2,8,128]{4,3,2,1,0:T(8,128)S(1)} %get-tuple-element.272), channel_id=1, source_target_pairs={{0,16},{16,32},{32,48},{48,64},{64,80},{80,96},{96,112},{1,17},{17... | collective-permute-start | bytes 147464 | tf_op jit(solution)/shard_map/ppermute | solution.py:27
  239.0 6.0 %collective-permute-start.20 = (f32[2,3,2,8,128]{4,3,2,1,0:T(8,128)S(1)}, f32[2,3,2,8,128]{4,3,2,1,0:T(8,128)S(1)}, u32[]{:S(2)}, u32[]{:S(2)}) collective-permute-start(f32[2,3,2,8,128]{4,3,2,1,0:T(8,128)S(1)} %get-tuple-element.273), channel_id=1, source_target_pairs={{16,0},{32,16},{48,32},{64,48},{80,64},{96,80},{112,96},{17,1},{33... | collective-permute-start | bytes 147464 | tf_op jit(solution)/shard_map/ppermute | solution.py:28
  240.3 4.7 %collective-permute-start.23 = (f32[2,3,16,2,128]{4,3,2,1,0:T(2,128)S(1)}, f32[2,3,16,2,128]{4,3,2,1,0:T(2,128)S(1)}, u32[]{:S(2)}, u32[]{:S(2)}) collective-permute-start(f32[2,3,16,2,128]{4,3,2,1,0:T(2,128)S(1)} %get-tuple-element.274), channel_id=1, source_target_pairs={{0,1},{1,2},{2,3},{3,4},{4,5},{5,6},{6,7},{7,8},{8,9},{9,10},{10,1... | collective-permute-start | bytes 294920 | tf_op jit(solution)/shard_map/ppermute | solution.py:27
  242.1 3.2 collective-permute-start.22
  289.4 9.3 %copy-start.2 = (f32[1,3,16,8,128]{4,3,2,1,0:T(8,128)}, f32[1,3,16,8,128]{4,3,2,1,0:T(8,128)S(1)}, u32[]{:S(2)}) copy-start(f32[1,3,16,8,128]{4,3,2,1,0:T(8,128)S(1)} %multiply_add_fusion.8) | copy-start | bytes 589828
  289.6 6.7 %collective-permute-start.25 = (f32[2,3,2,8,128]{4,3,2,1,0:T(8,128)S(1)}, f32[2,3,2,8,128]{4,3,2,1,0:T(8,128)S(1)}, u32[]{:S(2)}, u32[]{:S(2)}) collective-permute-start(f32[2,3,2,8,128]{4,3,2,1,0:T(8,128)S(1)} %get-tuple-element.266), channel_id=1, source_target_pairs={{0,16},{16,32},{32,48},{48,64},{64,80},{80,96},{96,112},{1,17},{17... | collective-permute-start | bytes 147464 | tf_op jit(solution)/shard_map/ppermute | solution.py:27
  291.9 6.0 %collective-permute-start.24 = (f32[2,3,2,8,128]{4,3,2,1,0:T(8,128)S(1)}, f32[2,3,2,8,128]{4,3,2,1,0:T(8,128)S(1)}, u32[]{:S(2)}, u32[]{:S(2)}) collective-permute-start(f32[2,3,2,8,128]{4,3,2,1,0:T(8,128)S(1)} %get-tuple-element.267), channel_id=1, source_target_pairs={{16,0},{32,16},{48,32},{64,48},{80,64},{96,80},{112,96},{17,1},{33... | collective-permute-start | bytes 147464 | tf_op jit(solution)/shard_map/ppermute | solution.py:28
  293.2 4.7 %collective-permute-start.27 = (f32[2,3,16,2,128]{4,3,2,1,0:T(2,128)S(1)}, f32[2,3,16,2,128]{4,3,2,1,0:T(2,128)S(1)}, u32[]{:S(2)}, u32[]{:S(2)}) collective-permute-start(f32[2,3,16,2,128]{4,3,2,1,0:T(2,128)S(1)} %get-tuple-element.268), channel_id=1, source_target_pairs={{0,1},{1,2},{2,3},{3,4},{4,5},{5,6},{6,7},{7,8},{8,9},{9,10},{10,1... | collective-permute-start | bytes 294920 | tf_op jit(solution)/shard_map/ppermute | solution.py:27
  295.1 3.7 collective-permute-start.26
  348.2 7.0 %collective-permute-start.29 = (f32[2,3,2,8,128]{4,3,2,1,0:T(8,128)S(1)}, f32[2,3,2,8,128]{4,3,2,1,0:T(8,128)S(1)}, u32[]{:S(2)}, u32[]{:S(2)}) collective-permute-start(f32[2,3,2,8,128]{4,3,2,1,0:T(8,128)S(1)} %get-tuple-element.258), channel_id=1, source_target_pairs={{0,16},{16,32},{32,48},{48,64},{64,80},{80,96},{96,112},{1,17},{17... | collective-permute-start | bytes 147464 | tf_op jit(solution)/shard_map/ppermute | solution.py:27
  350.6 6.0 %collective-permute-start.28 = (f32[2,3,2,8,128]{4,3,2,1,0:T(8,128)S(1)}, f32[2,3,2,8,128]{4,3,2,1,0:T(8,128)S(1)}, u32[]{:S(2)}, u32[]{:S(2)}) collective-permute-start(f32[2,3,2,8,128]{4,3,2,1,0:T(8,128)S(1)} %get-tuple-element.259), channel_id=1, source_target_pairs={{16,0},{32,16},{48,32},{64,48},{80,64},{96,80},{112,96},{17,1},{33... | collective-permute-start | bytes 147464 | tf_op jit(solution)/shard_map/ppermute | solution.py:28
  351.9 4.7 %collective-permute-start.31 = (f32[2,3,16,2,128]{4,3,2,1,0:T(2,128)S(1)}, f32[2,3,16,2,128]{4,3,2,1,0:T(2,128)S(1)}, u32[]{:S(2)}, u32[]{:S(2)}) collective-permute-start(f32[2,3,16,2,128]{4,3,2,1,0:T(2,128)S(1)} %get-tuple-element.260), channel_id=1, source_target_pairs={{0,1},{1,2},{2,3},{3,4},{4,5},{5,6},{6,7},{7,8},{8,9},{9,10},{10,1... | collective-permute-start | bytes 294920 | tf_op jit(solution)/shard_map/ppermute | solution.py:27
  353.7 3.2 collective-permute-start.30
  358.7 39.4 %copy-start.44 = (f32[3]{0:T(128)S(1)}, f32[3]{0:T(128)}, u32[]{:S(2)}) copy-start(f32[3]{0:T(128)} %get-tuple-element.151) | copy-start | bytes 40
  358.7 39.4 %copy-start.45 = (f32[3]{0:T(128)S(1)}, f32[3]{0:T(128)}, u32[]{:S(2)}) copy-start(f32[3]{0:T(128)} %get-tuple-element.152) | copy-start | bytes 40
  402.2 6.7 %collective-permute-start.33 = (f32[2,3,2,8,128]{4,3,2,1,0:T(8,128)S(1)}, f32[2,3,2,8,128]{4,3,2,1,0:T(8,128)S(1)}, u32[]{:S(2)}, u32[]{:S(2)}) collective-permute-start(f32[2,3,2,8,128]{4,3,2,1,0:T(8,128)S(1)} %get-tuple-element.252), channel_id=1, source_target_pairs={{0,16},{16,32},{32,48},{48,64},{64,80},{80,96},{96,112},{1,17},{17... | collective-permute-start | bytes 147464 | tf_op jit(solution)/shard_map/ppermute | solution.py:27
  404.4 6.0 %collective-permute-start.32 = (f32[2,3,2,8,128]{4,3,2,1,0:T(8,128)S(1)}, f32[2,3,2,8,128]{4,3,2,1,0:T(8,128)S(1)}, u32[]{:S(2)}, u32[]{:S(2)}) collective-permute-start(f32[2,3,2,8,128]{4,3,2,1,0:T(8,128)S(1)} %get-tuple-element.253), channel_id=1, source_target_pairs={{16,0},{32,16},{48,32},{64,48},{80,64},{96,80},{112,96},{17,1},{33... | collective-permute-start | bytes 147464 | tf_op jit(solution)/shard_map/ppermute | solution.py:28
  405.8 4.7 %collective-permute-start.35 = (f32[2,3,16,2,128]{4,3,2,1,0:T(2,128)S(1)}, f32[2,3,16,2,128]{4,3,2,1,0:T(2,128)S(1)}, u32[]{:S(2)}, u32[]{:S(2)}) collective-permute-start(f32[2,3,16,2,128]{4,3,2,1,0:T(2,128)S(1)} %get-tuple-element.254), channel_id=1, source_target_pairs={{0,1},{1,2},{2,3},{3,4},{4,5},{5,6},{6,7},{7,8},{8,9},{9,10},{10,1... | collective-permute-start | bytes 294920 | tf_op jit(solution)/shard_map/ppermute | solution.py:27
  407.6 3.7 collective-permute-start.34
  413.1 42.6 %copy-start.4 = (f32[1,3,16,8,128]{4,3,2,1,0:T(8,128)S(1)}, f32[1,3,16,8,128]{4,3,2,1,0:T(8,128)}, u32[]{:S(2)}) copy-start(f32[1,3,16,8,128]{4,3,2,1,0:T(8,128)} %copy-done.2) | copy-start | bytes 589828
  413.1 42.6 %copy-start.8 = (f32[1,3,16,8,128]{4,3,2,1,0:T(8,128)S(1)}, f32[1,3,16,8,128]{4,3,2,1,0:T(8,128)}, u32[]{:S(2)}) copy-start(f32[1,3,16,8,128]{4,3,2,1,0:T(8,128)} %copy-done.7) | copy-start | bytes 589828
  413.3 42.3 %copy-start.10 = (f32[1,3,16,8,128]{4,3,2,1,0:T(8,128)S(1)}, f32[1,3,16,8,128]{4,3,2,1,0:T(8,128)}, u32[]{:S(2)}) copy-start(f32[1,3,16,8,128]{4,3,2,1,0:T(8,128)} %copy-done.9) | copy-start | bytes 589828
  (34 other events, 53.7 us)
where the time goes:
time: 462 us; the launch traced here: 459 us
  blocking collectives  319 us (69%)
  starting transfers between devices  67.2 us (15%)
  other arithmetic  44.2 us (10%)
  waiting for transfers between devices  17.8 us (4%)
  local copies, waits for them, and re-layouts  9.09 us (2%)
    psum x24, blocking collectives, by_axis(): array = lax.psum(array, axis)  319 us
    ppermute x18, starting transfers between devices, padded_2(): lax.ppermute(last, axis, up)  43.8 us
    ppermute x18, starting transfers between devices, padded_2(): lax.ppermute(leading, axis, [(b, a) for a, b in up])  23.5 us
    ppermute x18, waiting for transfers between devices, padded_2(): lax.ppermute(leading, axis, [(b, a) for a, b in up])  17.7 us
    sub x11, other arithmetic, scale_complex(): real_coef * vector[0] - imag_coef * vector[1]  12.4 us
    concatenate x17, other arithmetic, padded_2(): jnp.concatenate([jnp.pad(low, around), array, jnp.pad(high, around)], axi...  10.2 us
  transfers between devices with their start and end apart: 36, of which 16 were waited for; matrix products, arithmetic and copies ran while one was open for 1% of the time, Pallas kernels for 0%

commit v1 on v0

v1 whole, which is shorter than its diff:
```python
import functools

import jax
import jax.numpy as jnp
from jax import lax
from jax.experimental import pallas as pl
from jax.experimental.pallas import tpu as pltpu
from jax.sharding import PartitionSpec as P

ITERS = 4
NB = 2 * ITERS + 1
SPACING = 0.25
HALF_STEP = 0.05
DIAG = 3.75 / SPACING**2
KAPPA = -0.5 / SPACING**2 * HALF_STEP * (4.0 / 3.0)
FAR = -1.0 / 16.0
MESH = pl.DeviceIdType.MESH
ROW = 8
IM = 64


def tri(i, j):
    return j * (j + 1) // 2 + i


def cmul(a, b):
    return (a[0] * b[0] - a[1] * b[1], a[0] * b[1] + a[1] * b[0])


def cconjmul(a, b):
    return (a[0] * b[0] + a[1] * b[1], a[0] * b[1] - a[1] * b[0])


def cdiv(a, b):
    modulus = b[0] * b[0] + b[1] * b[1]
    return ((a[0] * b[0] + a[1] * b[1]) / modulus, (a[1] * b[0] - a[0] * b[1]) / modulus)


def cadd(a, b):
    return (a[0] + b[0], a[1] + b[1])


def csub(a, b):
    return (a[0] - b[0], a[1] - b[1])


def csum(terms):
    while len(terms) > 1:
        terms = [cadd(terms[k], terms[k + 1]) if k + 1 < len(terms) else terms[k] for k in range(0, len(terms), 2)]
    return terms[0]


def shifted_sum(a):
    out = [a[0]]
    for k in range(1, len(a)):
        out.append(cadd(a[k], a[k - 1]))
    out.append(a[-1])
    return out


def axpy(a, s, b):
    out = []
    for k in range(max(len(a), len(b))):
        if k >= len(b):
            out.append(a[k])
        else:
            t = cmul(s, b[k])
            out.append(csub(a[k], t) if k < len(a) else (-t[0], -t[1]))
    return out


def recurrences(gram):
    def shadow_dot(a):
        return csum([cmul(gram(0, k), a[k]) for k in range(len(a))])

    one = jnp.ones_like(gram(0, 0)[0])
    zero = jnp.zeros_like(one)
    residual = [(one, zero)]
    direction = residual
    x = []
    rho = gram(0, 0)
    for iteration in range(ITERS):
        image = shifted_sum(direction)
        alpha = cdiv(rho, shadow_dot(image))
        half = axpy(residual, alpha, image)
        second = shifted_sum(half)
        n = len(second)
        g_second = [csum([cmul(gram(k, l), second[l]) for l in range(n)]) for k in range(n)]
        norm = csum([cconjmul(second[k], g_second[k]) for k in range(n)])[0]
        cross = csum([cconjmul(g_second[k], half[k]) for k in range(len(half))])
        omega = (cross[0] / norm, cross[1] / norm)
        minus = lambda s: (-s[0], -s[1])
        x = axpy(axpy(x, minus(alpha), direction), minus(omega), half)
        residual = axpy(half, omega, second)
        if iteration + 1 < ITERS:
            rho_next = shadow_dot(residual)
            beta = cmul(cdiv(rho_next, rho), cdiv(alpha, omega))
            direction = axpy(residual, minus(beta), axpy(direction, omega, image))
            rho = rho_next
    return residual, x


def kernel(
    nx, ny, orb_hbm, pot_ref, evolved_ref, residual_ref,
    u, w, pr, pi, gram, part_y, part_x, coef,
    load_sem, send_sem, recv_sem, ysend_sem, yrecv_sem, xsend_sem, xrecv_sem,
):
    norb, bx = orb_hbm.shape[1], orb_hbm.shape[2]
    io, ix, iy = lax.axis_index("orb"), lax.axis_index("gx"), lax.axis_index("gyz")
    rows = pl.ds(ROW, 8)

    loads = [
        pltpu.make_async_copy(orb_hbm.at[c, o], u.at[0, o, pl.ds(2, bx), c, rows], load_sem.at[o, c])
        for o in range(norb) for c in range(2)
    ]
    for copy in loads:
        copy.start()

    barrier = pltpu.get_barrier_semaphore()
    for d in range(1, ny):
        pl.semaphore_signal(barrier, inc=1, device_id=(io, ix, lax.rem(iy + d, ny)), device_id_type=MESH)
    for d in range(1, nx):
        pl.semaphore_signal(barrier, inc=1, device_id=(io, lax.rem(ix + d, nx), iy), device_id_type=MESH)

    everything = pl.ds(2, bx)
    sides = (
        (ix < nx - 1, (pl.ds(bx, 2), rows), (pl.ds(0, 2), rows), (io, ix + 1, iy), ix > 0),
        (ix > 0, (pl.ds(2, 2), rows), (pl.ds(bx + 2, 2), rows), (io, ix - 1, iy), ix < nx - 1),
        (iy < ny - 1, (everything, pl.ds(ROW + 6, 2)), (everything, pl.ds(ROW - 2, 2)), (io, ix, iy + 1), iy > 0),
        (iy > 0, (everything, pl.ds(ROW, 2)), (everything, pl.ds(ROW + 8, 2)), (io, ix, iy - 1), iy < ny - 1),
    )

    def halo(s, o, side):
        _, (sx, sr), (dx, dr), target, _ = sides[side]
        return pltpu.make_async_remote_copy(
            src_ref=u.at[s, o, sx, :, sr],
            dst_ref=u.at[s, o, dx, :, dr],
            send_sem=send_sem.at[s, o, side],
            recv_sem=recv_sem.at[s, o, side],
            device_id=target,
            device_id_type=MESH,
        )

    def send(s, o):
        for side in range(4):
            @pl.when(sides[side][0])
            def _():
                halo(s, o, side).start()

    def receive(s, o):
        for side in range(4):
            @pl.when(sides[side][4])
            def _():
                halo(s, o, side).wait_recv()

    def clear(side, _x, _r):
        @pl.when(jnp.logical_not(sides[side][4]))
        def _():
            def body(s, carry):
                for o in range(norb):
                    shape = (_x.size, 2, _r.size, 128)
                    u[s, o, _x, :, _r, :] = jnp.zeros(shape, jnp.float32)
                return carry
            lax.fori_loop(0, NB, body, 0)

    for side in range(4):
        clear(side, *sides[side][2])
    gram[...] = jnp.zeros_like(gram)

    def coefficients(x, carry):
        q = HALF_STEP * (DIAG + pot_ref[x])
        p = KAPPA / (1.0 + q * q)
        pr[x] = p
        pi[x] = -q * p
        return carry

    lax.fori_loop(0, bx, coefficients, 0, unroll=4)

    for copy in loads:
        copy.wait()
    pl.semaphore_wait(barrier, nx + ny - 2)
    for o in range(norb):
        send(0, o)

    lane = lax.broadcasted_iota(jnp.int32, (8, 128), 1)
    one, zero = jnp.float32(1.0), jnp.float32(0.0)
    near = (jnp.where(lane >= 1, one, zero), jnp.where(lane < 127, one, zero))
    far = (jnp.where(lane >= 2, FAR * one, zero), jnp.where(lane < 126, FAR * one, zero))

    def stencil(s, o, x, c):
        center = u[s, o, x + 2, c, rows]
        s1 = (u[s, o, x + 1, c, rows] + u[s, o, x + 3, c, rows]) + (
            u[s, o, x + 2, c, pl.ds(ROW - 1, 8)] + u[s, o, x + 2, c, pl.ds(ROW + 1, 8)]
        )
        s2 = (u[s, o, x, c, rows] + u[s, o, x + 4, c, rows]) + (
            u[s, o, x + 2, c, pl.ds(ROW - 2, 8)] + u[s, o, x + 2, c, pl.ds(ROW + 2, 8)]
        )
        z1 = near[0] * pltpu.roll(center, 1, 1) + near[1] * pltpu.roll(center, 127, 1)
        z2 = far[0] * pltpu.roll(center, 2, 1) + far[1] * pltpu.roll(center, 126, 1)
        return center, (s1 + z1) + (FAR * s2 + z2)

    def advance(s, o, first, last):
        def body(x, carry):
            c_re, t_re = stencil(s, o, x, 0)
            c_im, t_im = stencil(s, o, x, 1)
            if first:
                q = HALF_STEP * (DIAG + pot_ref[x])
                w_re = 2.0 * (KAPPA * t_im + q * c_im)
                w_im = -2.0 * (KAPPA * t_re + q * c_re)
            else:
                w_re, w_im = -t_im, t_re
            w[s, o, x, 0] = w_re
            w[s, o, x, 1] = w_im
            if not last:
                a, b = pr[x], pi[x]
                u[s + 1, o, x + 2, 0, rows] = a * w_re - b * w_im
                u[s + 1, o, x + 2, 1, rows] = a * w_im + b * w_re
            return carry
        lax.fori_loop(0, bx, body, 0, unroll=4)

    def products(s):
        def orbital(o, carry):
            def pair(i, carry):
                re, im = [], []
                for x in range(bx):
                    ar, ai, br, bi = w[i, o, x, 0], w[i, o, x, 1], w[s, o, x, 0], w[s, o, x, 1]
                    re.append(ar * br + ai * bi)
                    im.append(ar * bi - ai * br)
                row = s * (s + 1) // 2 + i
                for offset, terms in ((0, re), (IM, im)):
                    while len(terms) > 1:
                        terms = [terms[k] + terms[k + 1] for k in range(0, len(terms), 2)]
                    gram[o, pl.ds(offset + row, 1)] = jnp.sum(terms[0], axis=0, keepdims=True)
                return carry
            lax.fori_loop(0, s + 1, pair, 0)
            return carry
        lax.fori_loop(0, norb, orbital, 0)

    def step(s, first=False, last=False):
        for o in range(norb):
            receive(s, o)
            advance(s, o, first, last)
            if not last:
                send(s + 1, o)
        products(s)

    step(0, first=True)

    def middle(s, carry):
        step(s)
        return carry

    lax.fori_loop(1, NB - 1, middle, 0)
    step(NB - 1, last=True)

    ones = jnp.ones((8, 128), jnp.float32)
    row = lax.broadcasted_iota(jnp.int32, (8, 128), 0)
    mine = jnp.zeros((8, 128), jnp.float32)
    for o in range(norb):
        total = lax.dot_general(
            ones, gram[o], (((1,), (1,)), ((), ())),
            precision=lax.Precision.HIGHEST, preferred_element_type=jnp.float32,
        )
        mine = jnp.where(row == o, total, mine)

    def gather(part, me, n, target, ssem, rsem):
        def copy(d, slot):
            return pltpu.make_async_remote_copy(
                src_ref=part.at[me], dst_ref=part.at[slot],
                send_sem=ssem.at[d], recv_sem=rsem.at[slot],
                device_id=target(lax.rem(me + d, n)), device_id_type=MESH,
            )
        for d in range(1, n):
            copy(d, me).start()
        for d in range(1, n):
            copy(d, lax.rem(me + d, n)).wait_recv()
        for d in range(1, n):
            copy(d, me).wait_send()
        terms = [part[k] for k in range(n)]
        while len(terms) > 1:
            terms = [terms[k] + terms[k + 1] for k in range(0, len(terms), 2)]
        return terms[0]

    part_y[iy] = mine
    line = gather(part_y, iy, ny, lambda t: (io, ix, t), ysend_sem, yrecv_sem)
    part_x[ix] = line
    total = gather(part_x, ix, nx, lambda t: (io, t, iy), xsend_sem, xrecv_sem)

    def spread(e):
        return jnp.broadcast_to(total[:, e:e + 1], (8, 128))

    entries = {}
    for j in range(NB):
        for i in range(j + 1):
            re = spread(tri(i, j))
            im = jnp.zeros_like(re) if i == j else spread(IM + tri(i, j))
            entries[i, j] = (re, im)
            if i != j:
                entries[j, i] = (re, -im)
    res_coef, x_coef = recurrences(lambda i, j: entries[i, j])
    for k in range(NB):
        coef[0, k, 0], coef[0, k, 1] = res_coef[k]
        if k < NB - 1:
            coef[1, k, 0] = x_coef[k][0] * (1.0 / KAPPA)
            coef[1, k, 1] = x_coef[k][1] * (1.0 / KAPPA)

    for o in range(norb):
        def take(kind, k, c):
            return jnp.broadcast_to(coef[kind, k, c, pl.ds(o, 1)], (8, 128))

        rc = [(take(0, k, 0), take(0, k, 1)) for k in range(NB)]
        xc = [(take(1, k, 0), take(1, k, 1)) for k in range(NB - 1)]

        def combine(x, carry):
            vectors = [(w[k, o, x, 0], w[k, o, x, 1]) for k in range(NB)]
            res = csum([cmul(rc[k], vectors[k]) for k in range(NB)])
            inc = csum([cmul(xc[k], vectors[k]) for k in range(NB - 1)])
            inc = cmul((pr[x], pi[x]), inc)
            for c in range(2):
                residual_ref[c, o, x] = res[c]
                evolved_ref[c, o, x] = u[0, o, x + 2, c, rows] + inc[c]
            return carry

        lax.fori_loop(0, bx, combine, 0)

    def drain(s, carry):
        for o in range(norb):
            for side in range(4):
                @pl.when(sides[side][0])
                def _():
                    halo(s, o, side).wait_send()
        return carry

    lax.fori_loop(0, NB, drain, 0)


def solution(mesh):
    nx, ny = mesh.shape["gx"], mesh.shape["gyz"]

    def shards(orbitals, potential):
        _, norb, bx, by, nz = orbitals.shape
        block = jax.ShapeDtypeStruct(orbitals.shape, jnp.float32)
        return pl.pallas_call(
            functools.partial(kernel, nx, ny),
            out_shape=(block, block),
            in_specs=[pl.BlockSpec(memory_space=pl.ANY), pl.BlockSpec(memory_space=pltpu.VMEM)],
            out_specs=(pl.BlockSpec(memory_space=pltpu.VMEM), pl.BlockSpec(memory_space=pltpu.VMEM)),
            scratch_shapes=[
                pltpu.VMEM((NB, norb, bx + 4, 2, by + 16, nz), jnp.float32),
                pltpu.VMEM((NB, norb, bx, 2, by, nz), jnp.float32),
                pltpu.VMEM((bx, by, nz), jnp.float32),
                pltpu.VMEM((bx, by, nz), jnp.float32),
                pltpu.VMEM((norb, 128, 128), jnp.float32),
                pltpu.VMEM((ny, 8, 128), jnp.float32),
                pltpu.VMEM((nx, 8, 128), jnp.float32),
                pltpu.VMEM((2, NB, 2, 8, 128), jnp.float32),
                pltpu.SemaphoreType.DMA((norb, 2)),
                pltpu.SemaphoreType.DMA((NB, norb, 4)),
                pltpu.SemaphoreType.DMA((NB, norb, 4)),
                pltpu.SemaphoreType.DMA((ny,)),
                pltpu.SemaphoreType.DMA((ny,)),
                pltpu.SemaphoreType.DMA((nx,)),
                pltpu.SemaphoreType.DMA((nx,)),
            ],
            compiler_params=pltpu.CompilerParams(
                collective_id=0, has_side_effects=True, vmem_limit_bytes=48 * 2**20
            ),
        )(orbitals, potential)

    spec = P(None, "orb", "gx", "gyz", None)
    return jax.shard_map(
        shards, mesh=mesh, in_specs=(spec, P("gx", "gyz", None)), out_specs=(spec, spec), check_vma=False
    )
```

time: 462 us -> 68.4 us (0.15)
  blocking collectives: 319 us -> 0 us
  starting transfers between devices: 67.2 us -> 0 us
  Pallas kernels: 0 us -> 64 us
  other arithmetic: 44.2 us -> 0 us
  waiting for transfers between devices: 17.8 us -> 0 us
  local copies, waits for them, and re-layouts: 9.09 us -> 3.32 us
    psum x24 -> x0, blocking collectives: 319 us -> none  [by_axis(): array = lax.psum(array, axis)]
    ppermute x36 -> x0, starting transfers between devices: 67.2 us -> none  [the longest x18 43.8 us: padded_2(): lax.ppermute(last, axis, up)]
    pallas_call x0 -> x1, Pallas kernels: none -> 64 us  [shards(): pl.pallas_call(functools.partial(kernel, nx, ny), out_shape=(block, block...]
    sub x29 -> x0, other arithmetic: 19.9 us -> none  [the longest x11 12.4 us: scale_complex(): real_coef * vector[0] - imag_coef * vector[1]]
    ppermute x36 -> x0, waiting for transfers between devices: 17.8 us -> none  [the longest x18 17.7 us: padded_2(): lax.ppermute(leading, axis, [(b, a) for a, b in up])]
    concatenate x17 -> x0, other arithmetic: 10.2 us -> none  [padded_2(): jnp.concatenate([jnp.pad(low, around), array, jnp.pad(high, around)], axi...]
    add x22 -> x0, other arithmetic: 7.61 us -> none  [the longest x9 5.72 us: laplace_apply(): return -0.5 / SPACING ** 2 * summed + potential * center]
  transfers between devices with their start and end apart: 36 -> 0, of which waited for: 16 -> 0; matrix products, arithmetic and copies ran while one was open for 1% -> 0% of each run, Pallas kernels for 0% -> 0%
where the time goes in v1:
time: 68.4 us; the launch traced here: 68 us
  Pallas kernels  64 us (94%)
  local copies, waits for them, and re-layouts  3.32 us (5%)
    pallas_call x1, Pallas kernels, shards(): pl.pallas_call(functools.partial(kernel, nx, ny), out_shape=(block, block...  64 us
    unnamed x6, local copies, waits for them, and re-layouts  3.32 us

profile of v1, /device:TPU:6, one launch (start us, length us, event | category | flops | bytes accessed | tf_op | source)
XLA Modules:
  0.0 68.0 jit_solution(4088344726927795267)
XLA Ops:
  0.6 0.0 copy-start
  0.6 1.0 %copy-done = f32[2,3,16,8,128]{4,3,2,1,0:T(8,128)S(1)} copy-done((f32[2,3,16,8,128]{4,3,2,1,0:T(8,128)S(1)}, f32[2,3,16,8,128]{4,3,2,1,0:T(8,128)}, u32[]{:S(2)}) %copy-start) | copy-done | bytes 393240
  1.6 0.0 copy-start.1
  1.6 0.8 %copy-done.1 = f32[16,8,128]{2,1,0:T(8,128)S(1)} copy-done((f32[16,8,128]{2,1,0:T(8,128)S(1)}, f32[16,8,128]{2,1,0:T(8,128)}, u32[]{:S(2)}) %copy-start.1) | copy-done | bytes 65560
  2.5 64.0 %shard_map.41 = (f32[2,3,16,8,128]{4,3,2,1,0:T(8,128)S(1)}, f32[2,3,16,8,128]{4,3,2,1,0:T(8,128)S(1)}) custom-call(f32[2,3,16,8,128]{4,3,2,1,0:T(8,128)S(1)} %copy-done, f32[16,8,128]{2,1,0:T(8,128)S(1)} %copy-done.1), custom_call_target="tpu_custom_call" | custom-call | tf_op jit(solution)/shard_map/pallas_call | solution.py:343
  66.5 0.7 %copy.6 = f32[2,3,16,8,128]{4,3,2,1,0:T(8,128)} copy(f32[2,3,16,8,128]{4,3,2,1,0:T(8,128)S(1)} %get-tuple-element.4) | data formatting | bytes 786432
  67.2 0.7 %copy.7 = f32[2,3,16,8,128]{4,3,2,1,0:T(8,128)} copy(f32[2,3,16,8,128]{4,3,2,1,0:T(8,128)S(1)} %get-tuple-element.5) | data formatting | bytes 786432
Async XLA Ops:
  0.6 1.0 %copy-start = (f32[2,3,16,8,128]{4,3,2,1,0:T(8,128)S(1)}, f32[2,3,16,8,128]{4,3,2,1,0:T(8,128)}, u32[]{:S(2)}) copy-start(f32[2,3,16,8,128]{4,3,2,1,0:T(8,128)} %orb_hbm.1) | copy-start | bytes 1179652
  1.6 0.8 %copy-start.1 = (f32[16,8,128]{2,1,0:T(8,128)S(1)}, f32[16,8,128]{2,1,0:T(8,128)}, u32[]{:S(2)}) copy-start(f32[16,8,128]{2,1,0:T(8,128)} %pot_ref.1) | copy-start | bytes 196612

commit v2 on v1

v2 whole, which is shorter than its diff:
```python
import functools

import jax
import jax.numpy as jnp
from jax import lax
from jax.experimental import pallas as pl
from jax.experimental.pallas import tpu as pltpu
from jax.sharding import PartitionSpec as P

ITERS = 4
NB = 2 * ITERS + 1
SPACING = 0.25
HALF_STEP = 0.05
DIAG = 3.75 / SPACING**2
KAPPA = -0.5 / SPACING**2 * HALF_STEP * (4.0 / 3.0)
FAR = -1.0 / 16.0
MESH = pl.DeviceIdType.MESH
GROUP = 3
WIDTH = 2 * GROUP
NEAR = WIDTH - 2
ROW = 8
RC = 4
IM = 64


_ANGLE = (0.955336489, 0.295520207)
_NODES = (0.0, 0.6761480, -0.6761480, 0.0, 0.1811733, -0.1811733, 0.0, 0.4949747, -0.4949747)
SHIFT = tuple((t * _ANGLE[0], t * _ANGLE[1]) for t in _NODES)


def tri(i, j):
    return j * (j + 1) // 2 + i


def cmul(a, b):
    return (a[0] * b[0] - a[1] * b[1], a[0] * b[1] + a[1] * b[0])


def cconjmul(a, b):
    return (a[0] * b[0] + a[1] * b[1], a[0] * b[1] - a[1] * b[0])


def cdiv(a, b):
    modulus = b[0] * b[0] + b[1] * b[1]
    return ((a[0] * b[0] + a[1] * b[1]) / modulus, (a[1] * b[0] - a[0] * b[1]) / modulus)


def cadd(a, b):
    return (a[0] + b[0], a[1] + b[1])


def csub(a, b):
    return (a[0] - b[0], a[1] - b[1])


def csum(terms):
    while len(terms) > 1:
        terms = [cadd(terms[k], terms[k + 1]) if k + 1 < len(terms) else terms[k] for k in range(0, len(terms), 2)]
    return terms[0]


def shifted_sum(a):
    out = []
    for k in range(len(a)):
        re, im = SHIFT[k + 1]
        t = a[k] if re == 0.0 else cmul((1.0 + re, im), a[k])
        out.append(cadd(t, a[k - 1]) if k else t)
    out.append(a[-1])
    return out


def axpy(a, s, b):
    out = []
    for k in range(max(len(a), len(b))):
        if k >= len(b):
            out.append(a[k])
        else:
            t = cmul(s, b[k])
            out.append(csub(a[k], t) if k < len(a) else (-t[0], -t[1]))
    return out


def recurrences(gram):
    def shadow_dot(a):
        return csum([cmul(gram(0, k), a[k]) for k in range(len(a))])

    one = jnp.ones_like(gram(0, 0)[0])
    zero = jnp.zeros_like(one)
    residual = [(one, zero)]
    direction = residual
    x = []
    rho = gram(0, 0)
    for iteration in range(ITERS):
        image = shifted_sum(direction)
        alpha = cdiv(rho, shadow_dot(image))
        half = axpy(residual, alpha, image)
        second = shifted_sum(half)
        n = len(second)
        g_second = [csum([cmul(gram(k, l), second[l]) for l in range(n)]) for k in range(n)]
        norm = csum([cconjmul(second[k], g_second[k]) for k in range(n)])[0]
        cross = csum([cconjmul(g_second[k], half[k]) for k in range(len(half))])
        omega = (cross[0] / norm, cross[1] / norm)
        minus = lambda s: (-s[0], -s[1])
        x = axpy(axpy(x, minus(alpha), direction), minus(omega), half)
        residual = axpy(half, omega, second)
        if iteration + 1 < ITERS:
            rho_next = shadow_dot(residual)
            beta = cmul(cdiv(rho_next, rho), cdiv(alpha, omega))
            direction = axpy(residual, minus(beta), axpy(direction, omega, image))
            rho = rho_next
    return residual, x


def kernel(
    nx, ny, orb_hbm, pot_hbm, evolved_ref, residual_ref, *scratch,
):
    us, ws = scratch[:NB], scratch[NB:2 * NB]
    (pot, pr, pi, qf, gram, part_y, part_x, coef,
     load_sem, pot_sem, send_sem, recv_sem, ysend_sem, yrecv_sem, xsend_sem, xrecv_sem) = scratch[2 * NB:]
    norb, bx = orb_hbm.shape[1], orb_hbm.shape[2]
    io, ix, iy = lax.axis_index("orb"), lax.axis_index("gx"), lax.axis_index("gyz")
    rows = pl.ds(ROW, 8)

    loads = [pltpu.make_async_copy(pot_hbm, pot.at[pl.ds(NEAR, bx), rows], load_sem.at[2 * norb])] + [
        pltpu.make_async_copy(orb_hbm.at[c, o], us[0].at[o, pl.ds(WIDTH, bx), c, rows], load_sem.at[2 * o + c])
        for o in range(norb) for c in range(2)
    ]
    for copy in loads:
        copy.start()

    low_x, high_x, low_y, high_y = ix > 0, ix < nx - 1, iy > 0, iy < ny - 1
    exists = {-1: (low_x, low_y), 0: (None, None), 1: (high_x, high_y)}

    def present(dx, dy):
        a, b = exists[dx][0], exists[dy][1]
        return b if a is None else a if b is None else jnp.logical_and(a, b)

    sides = ((1, 0), (-1, 0), (0, 1), (0, -1), (1, 1), (1, -1), (-1, 1), (-1, -1))

    def span(d, length, first, width):
        if d == 0:
            return pl.ds(first, length), pl.ds(first, length)
        if d > 0:
            return pl.ds(first + length - width, width), pl.ds(first - width, width)
        return pl.ds(first, width), pl.ds(first + length, width)

    barrier = pltpu.get_barrier_semaphore()
    for d in range(1, ny):
        pl.semaphore_signal(barrier, inc=1, device_id=(io, ix, lax.rem(iy + d, ny)), device_id_type=MESH)
    for d in range(1, nx):
        pl.semaphore_signal(barrier, inc=1, device_id=(io, lax.rem(ix + d, nx), iy), device_id_type=MESH)
    expected = nx + ny - 2
    for dx, dy in sides[4:]:
        @pl.when(present(dx, dy))
        def _():
            pl.semaphore_signal(barrier, inc=1, device_id=(io, ix + dx, iy + dy), device_id_type=MESH)
        expected = expected + present(dx, dy).astype(jnp.int32)

    def pot_halo(side):
        dx, dy = sides[side]
        (sx, tx), (sr, tr) = span(dx, bx, NEAR, NEAR), span(dy, 8, ROW, NEAR)
        return pltpu.make_async_remote_copy(
            src_ref=pot.at[sx, sr], dst_ref=pot.at[tx, tr],
            send_sem=pot_sem.at[0, side], recv_sem=pot_sem.at[1, side],
            device_id=(io, ix + dx, iy + dy), device_id_type=MESH,
        )

    def halo(g, o, side):
        dx, dy = sides[side]
        width = NEAR if dx and dy else WIDTH
        (sx, tx), (sr, tr) = span(dx, bx, WIDTH, width), span(dy, 8, ROW, width)
        ref = us[GROUP * g]
        return pltpu.make_async_remote_copy(
            src_ref=ref.at[o, sx, :, sr], dst_ref=ref.at[o, tx, :, tr],
            send_sem=send_sem.at[g, o, side], recv_sem=recv_sem.at[g, o, side],
            device_id=(io, ix + dx, iy + dy), device_id_type=MESH,
        )

    def each_side(sent, act):
        for side, (dx, dy) in enumerate(sides):
            @pl.when(present(dx, dy) if sent else present(-dx, -dy))
            def _():
                act(side)

    def send(g, o):
        each_side(True, lambda side: halo(g, o, side).start())

    def receive(g, o):
        each_side(False, lambda side: halo(g, o, side).wait_recv())

    def clear(x0, nplanes, r0, nrows):
        def body(x, carry):
            for g in range(NB // GROUP):
                for o in range(norb):
                    us[GROUP * g][o, x, :, pl.ds(r0, nrows), :] = jnp.zeros((2, nrows, 128), jnp.float32)
            return carry
        lax.fori_loop(x0, x0 + nplanes, body, 0)

    def clear_pot(x0, nplanes, r0, nrows):
        pot[pl.ds(x0, nplanes), pl.ds(r0, nrows), :] = jnp.zeros((nplanes, nrows, 128), jnp.float32)

    for has, x0 in ((low_x, 0), (high_x, bx + WIDTH)):
        @pl.when(jnp.logical_not(has))
        def _():
            clear(x0, WIDTH, ROW - WIDTH, 8 + 2 * WIDTH)
            clear_pot(0 if x0 == 0 else bx + NEAR, NEAR, ROW - NEAR, 8 + 2 * NEAR)
    for has, r0 in ((low_y, ROW - WIDTH), (high_y, ROW + 8)):
        @pl.when(jnp.logical_not(has))
        def _():
            clear(0, bx + 2 * WIDTH, r0, WIDTH)
            clear_pot(0, bx + 2 * NEAR, ROW - NEAR if r0 < ROW else ROW + 8, NEAR)
    gram[...] = jnp.zeros_like(gram)

    for copy in loads:
        copy.wait()
    pl.semaphore_wait(barrier, expected)
    each_side(True, lambda side: pot_halo(side).start())
    for o in range(norb):
        send(0, o)

    zero, one = jnp.float32(0.0), jnp.float32(1.0)
    row = lax.broadcasted_iota(jnp.int32, (8, 128), 0)
    keep_rows = (
        jnp.where(jnp.logical_or(row >= ROW - RC, low_y), one, zero),
        jnp.where(jnp.logical_or(row < 8 - (ROW - RC), high_y), one, zero),
    )

    def coefficients(x, keep):
        for t in range(2):
            q = HALF_STEP * (DIAG + pot[x, pl.ds(RC + 8 * t, 8)])
            p = KAPPA / (1.0 + q * q) * keep_rows[t] * keep
            tile = pl.ds(8 * t, 8)
            qf[x, tile] = q
            pr[x, tile] = p
            pi[x, tile] = -q * p

    each_side(False, lambda side: pot_halo(side).wait_recv())
    lax.fori_loop(0, NEAR, lambda x, c: (coefficients(x, jnp.where(low_x, one, zero)), c)[1], 0)
    lax.fori_loop(NEAR, bx + NEAR, lambda x, c: (coefficients(x, one), c)[1], 0, unroll=4)
    lax.fori_loop(bx + NEAR, bx + 2 * NEAR, lambda x, c: (coefficients(x, jnp.where(high_x, one, zero)), c)[1], 0)

    lane = lax.broadcasted_iota(jnp.int32, (8, 128), 1)
    near = (jnp.where(lane >= 1, one, zero), jnp.where(lane < 127, one, zero))
    far = (jnp.where(lane >= 2, FAR * one, zero), jnp.where(lane < 126, FAR * one, zero))

    def stencil(u, o, x, c, r):
        def at(dx, dr):
            return u[o, x + WIDTH + dx, c, pl.ds(r + dr, 8)]
        center = at(0, 0)
        s1 = (at(-1, 0) + at(1, 0)) + (at(0, -1) + at(0, 1))
        s2 = (at(-2, 0) + at(2, 0)) + (at(0, -2) + at(0, 2))
        z1 = near[0] * pltpu.roll(center, 1, 1) + near[1] * pltpu.roll(center, 127, 1)
        z2 = far[0] * pltpu.roll(center, 2, 1) + far[1] * pltpu.roll(center, 126, 1)
        return center, (s1 + z1) + (FAR * s2 + z2)

    def wrows(s):
        return pl.ds(ROW - RC, 8) if s % GROUP < GROUP - 1 else pl.ds(0, 8)

    def advance(s, o):
        u, margin = us[s], WIDTH - 2 - 2 * (s % GROUP)
        a_shift, b_shift = SHIFT[s][0] / KAPPA, SHIFT[s][1] / KAPPA
        for x in range(-margin, bx + margin):
            out = -x if x < 0 else x - bx + 1 if x >= bx else 0
            beyond = margin - 2 * ((out + 1) // 2)
            for r in (ROW,) if beyond == 0 else (RC, RC + 8):
                u_re, t_re = stencil(u, o, x, 0, r)
                u_im, t_im = stencil(u, o, x, 1, r)
                tile = pl.ds(r - RC, 8)
                if s == 0:
                    q = qf[x + NEAR, tile]
                    w_re = 2.0 * (KAPPA * t_im + q * u_im)
                    w_im = -2.0 * (KAPPA * t_re + q * u_re)
                elif a_shift == 0.0:
                    w_re, w_im = -t_im, t_re
                else:
                    q = qf[x + NEAR, tile]
                    a, b = a_shift - b_shift * q, b_shift + a_shift * q
                    w_re = b * u_im - (t_im + a * u_re)
                    w_im = t_re - (a * u_im + b * u_re)
                if 0 <= x < bx:
                    dest = pl.ds(r - RC, 8) if beyond else pl.ds(0, 8)
                    ws[s][o, x, 0, dest] = w_re
                    ws[s][o, x, 1, dest] = w_im
                if s < NB - 1:
                    a, b = pr[x + NEAR, tile], pi[x + NEAR, tile]
                    us[s + 1][o, x + WIDTH, 0, pl.ds(r, 8)] = a * w_re - b * w_im
                    us[s + 1][o, x + WIDTH, 1, pl.ds(r, 8)] = a * w_im + b * w_re

    def vector(s, o, x):
        return ws[s][o, x, 0, wrows(s)], ws[s][o, x, 1, wrows(s)]

    def products(o, pairs):
        acc = {}
        used = sorted({k for pair in pairs for k in pair})
        for x in range(bx):
            v = {k: vector(k, o, x) for k in used}
            for i, j in pairs:
                (ar, ai), (br, bi) = v[i], v[j]
                terms = [ar * br + ai * bi] + ([ar * bi - ai * br] if i != j else [])
                for part, term in enumerate(terms):
                    key = (i, j, part, x % 2)
                    acc[key] = acc[key] + term if key in acc else term
        for i, j in pairs:
            for part in range(1 if i == j else 2):
                tile = acc[i, j, part, 0] + acc[i, j, part, 1]
                gram[o, pl.ds(part * IM + tri(i, j), 1)] = jnp.sum(tile, axis=0, keepdims=True)

    def column_products(g, o):
        new = range(GROUP * g, GROUP * g + GROUP)
        for i in range(GROUP * g):
            products(o, [(i, j) for j in new])
        products(o, [(i, j) for i in new for j in new if i <= j][:3])
        products(o, [(i, j) for i in new for j in new if i <= j][3:])

    groups = NB // GROUP
    for g in range(groups):
        def orbital(o, carry):
            receive(g, o)
            for s in range(GROUP * g, GROUP * g + GROUP):
                advance(s, o)
            if g < groups - 1:
                send(g + 1, o)
            else:
                column_products(g, o)
            return carry
        lax.fori_loop(0, norb, orbital, 0)
        if g < groups - 1:
            def gram_columns(o, carry):
                column_products(g, o)
                return carry
            lax.fori_loop(0, norb, gram_columns, 0)

    ones = jnp.ones((8, 128), jnp.float32)
    mine = jnp.zeros((8, 128), jnp.float32)
    for o in range(norb):
        total = lax.dot_general(
            ones, gram[o], (((1,), (1,)), ((), ())),
            precision=lax.Precision.HIGHEST, preferred_element_type=jnp.float32,
        )
        mine = jnp.where(row == o, total, mine)

    def gather(part, me, n, target, ssem, rsem):
        def copy(d, slot):
            return pltpu.make_async_remote_copy(
                src_ref=part.at[me], dst_ref=part.at[slot],
                send_sem=ssem.at[d], recv_sem=rsem.at[slot],
                device_id=target(lax.rem(me + d, n)), device_id_type=MESH,
            )
        for d in range(1, n):
            copy(d, me).start()
        for d in range(1, n):
            copy(d, lax.rem(me + d, n)).wait_recv()
        for d in range(1, n):
            copy(d, me).wait_send()
        terms = [part[k] for k in range(n)]
        while len(terms) > 1:
            terms = [terms[k] + terms[k + 1] for k in range(0, len(terms), 2)]
        return terms[0]

    part_y[iy] = mine
    line = gather(part_y, iy, ny, lambda t: (io, ix, t), ysend_sem, yrecv_sem)
    part_x[ix] = line
    total = gather(part_x, ix, nx, lambda t: (io, t, iy), xsend_sem, xrecv_sem)

    def spread(e):
        return jnp.broadcast_to(total[:, e:e + 1], (8, 128))

    entries = {}
    for j in range(NB):
        for i in range(j + 1):
            re = spread(tri(i, j))
            im = jnp.zeros_like(re) if i == j else spread(IM + tri(i, j))
            entries[i, j] = (re, im)
            if i != j:
                entries[j, i] = (re, -im)
    res_coef, x_coef = recurrences(lambda i, j: entries[i, j])
    for k in range(NB):
        coef[0, k, 0], coef[0, k, 1] = res_coef[k]
        if k < NB - 1:
            coef[1, k, 0] = x_coef[k][0] * (1.0 / KAPPA)
            coef[1, k, 1] = x_coef[k][1] * (1.0 / KAPPA)

    for o in range(norb):
        def take(kind, k, c):
            return jnp.broadcast_to(coef[kind, k, c, pl.ds(o, 1)], (8, 128))

        rc = [(take(0, k, 0), take(0, k, 1)) for k in range(NB)]
        xc = [(take(1, k, 0), take(1, k, 1)) for k in range(NB - 1)]

        def combine(x, carry):
            vectors = [vector(k, o, x) for k in range(NB)]
            res = csum([cmul(rc[k], vectors[k]) for k in range(NB)])
            inc = csum([cmul(xc[k], vectors[k]) for k in range(NB - 1)])
            inside = pl.ds(ROW - RC, 8)
            inc = cmul((pr[x + NEAR, inside], pi[x + NEAR, inside]), inc)
            for c in range(2):
                residual_ref[c, o, x] = res[c]
                evolved_ref[c, o, x] = us[0][o, x + WIDTH, c, rows] + inc[c]
            return carry

        lax.fori_loop(0, bx, combine, 0)

    each_side(True, lambda side: pot_halo(side).wait_send())
    for g in range(groups):
        def drain(o, carry):
            each_side(True, lambda side: halo(g, o, side).wait_send())
            return carry
        lax.fori_loop(0, norb, drain, 0)


def solution(mesh):
    nx, ny = mesh.shape["gx"], mesh.shape["gyz"]

    def shards(orbitals, potential):
        _, norb, bx, by, nz = orbitals.shape
        block = jax.ShapeDtypeStruct(orbitals.shape, jnp.float32)
        return pl.pallas_call(
            functools.partial(kernel, nx, ny),
            out_shape=(block, block),
            in_specs=[pl.BlockSpec(memory_space=pltpu.HBM)] * 2,
            out_specs=(pl.BlockSpec(memory_space=pltpu.VMEM), pl.BlockSpec(memory_space=pltpu.VMEM)),
            scratch_shapes=[
                pltpu.VMEM((norb, bx + 2 * WIDTH, 2, by + 16, nz), jnp.float32) for _ in range(NB)
            ] + [
                pltpu.VMEM((norb, bx, 2, 16 if s % GROUP < GROUP - 1 else 8, nz), jnp.float32) for s in range(NB)
            ] + [
                pltpu.VMEM((bx + 2 * NEAR, by + 16, nz), jnp.float32),
                pltpu.VMEM((bx + 2 * NEAR, 16, nz), jnp.float32),
                pltpu.VMEM((bx + 2 * NEAR, 16, nz), jnp.float32),
                pltpu.VMEM((bx + 2 * NEAR, 16, nz), jnp.float32),
                pltpu.VMEM((norb, 128, 128), jnp.float32),
                pltpu.VMEM((ny, 8, 128), jnp.float32),
                pltpu.VMEM((nx, 8, 128), jnp.float32),
                pltpu.VMEM((2, NB, 2, 8, 128), jnp.float32),
                pltpu.SemaphoreType.DMA((2 * norb + 1,)),
                pltpu.SemaphoreType.DMA((2, 8)),
                pltpu.SemaphoreType.DMA((NB // GROUP, norb, 8)),
                pltpu.SemaphoreType.DMA((NB // GROUP, norb, 8)),
                pltpu.SemaphoreType.DMA((ny,)),
                pltpu.SemaphoreType.DMA((ny,)),
                pltpu.SemaphoreType.DMA((nx,)),
                pltpu.SemaphoreType.DMA((nx,)),
            ],
            compiler_params=pltpu.CompilerParams(
                collective_id=0, has_side_effects=True, vmem_limit_bytes=48 * 2**20
            ),
        )(orbitals, potential)

    spec = P(None, "orb", "gx", "gyz", None)
    return jax.shard_map(
        shards, mesh=mesh, in_specs=(spec, P("gx", "gyz", None)), out_specs=(spec, spec), check_vma=False
    )
```

time: 68.4 us -> 53.5 us (0.78)
  Pallas kernels: 64 us -> 49.1 us
    pallas_call x1, Pallas kernels: 64 us -> 49.1 us  [shards(): pl.pallas_call(functools.partial(kernel, nx, ny), out_shape=(block, block...]
where the time goes in v2:
time: 53.5 us; the launch traced here: 53.1 us
  Pallas kernels  49.1 us (92%)
  local copies, waits for them, and re-layouts  3.32 us (6%)
  between operations  0.65 us (1%)
    pallas_call x1, Pallas kernels, shards(): pl.pallas_call(functools.partial(kernel, nx, ny), out_shape=(block, block...  49.1 us
    unnamed x6, local copies, waits for them, and re-layouts  3.32 us

profile of v2, /device:TPU:6, one launch (start us, length us, event | category | flops | bytes accessed | tf_op | source)
XLA Modules:
  0.0 53.1 jit_solution(13651314235973895122)
XLA Ops:
  0.6 0.0 copy-start
  0.6 1.0 %copy-done = f32[2,3,16,8,128]{4,3,2,1,0:T(8,128)S(1)} copy-done((f32[2,3,16,8,128]{4,3,2,1,0:T(8,128)S(1)}, f32[2,3,16,8,128]{4,3,2,1,0:T(8,128)}, u32[]{:S(2)}) %copy-start) | copy-done | bytes 393240
  1.6 0.0 copy-start.1
  1.6 0.8 %copy-done.1 = f32[16,8,128]{2,1,0:T(8,128)S(1)} copy-done((f32[16,8,128]{2,1,0:T(8,128)S(1)}, f32[16,8,128]{2,1,0:T(8,128)}, u32[]{:S(2)}) %copy-start.1) | copy-done | bytes 65560
  2.5 49.1 %shard_map.41 = (f32[2,3,16,8,128]{4,3,2,1,0:T(8,128)S(1)}, f32[2,3,16,8,128]{4,3,2,1,0:T(8,128)S(1)}) custom-call(f32[2,3,16,8,128]{4,3,2,1,0:T(8,128)S(1)} %copy-done, f32[16,8,128]{2,1,0:T(8,128)S(1)} %copy-done.1), custom_call_target="tpu_custom_call" | custom-call | tf_op jit(solution)/shard_map/pallas_call | solution.py:417
  51.6 0.7 %copy.6 = f32[2,3,16,8,128]{4,3,2,1,0:T(8,128)} copy(f32[2,3,16,8,128]{4,3,2,1,0:T(8,128)S(1)} %get-tuple-element.4) | data formatting | bytes 786432
  52.3 0.7 %copy.7 = f32[2,3,16,8,128]{4,3,2,1,0:T(8,128)} copy(f32[2,3,16,8,128]{4,3,2,1,0:T(8,128)S(1)} %get-tuple-element.5) | data formatting | bytes 786432
Async XLA Ops:
  0.6 1.0 %copy-start = (f32[2,3,16,8,128]{4,3,2,1,0:T(8,128)S(1)}, f32[2,3,16,8,128]{4,3,2,1,0:T(8,128)}, u32[]{:S(2)}) copy-start(f32[2,3,16,8,128]{4,3,2,1,0:T(8,128)} %orb_hbm.1) | copy-start | bytes 1179652
  1.6 0.8 %copy-start.1 = (f32[16,8,128]{2,1,0:T(8,128)S(1)}, f32[16,8,128]{2,1,0:T(8,128)}, u32[]{:S(2)}) copy-start(f32[16,8,128]{2,1,0:T(8,128)} %pot_hbm.1) | copy-start | bytes 196612

commit v3 on v2

--- a/solution.py
+++ b/solution.py
@@ -116,7 +116,7 @@
 ):
     us, ws = scratch[:NB], scratch[NB:2 * NB]
     (pot, pr, pi, qf, gram, part_y, part_x, coef,
-     load_sem, pot_sem, send_sem, recv_sem, ysend_sem, yrecv_sem, xsend_sem, xrecv_sem) = scratch[2 * NB:]
+     ready, load_sem, pot_sem, send_sem, recv_sem, ysend_sem, yrecv_sem, xsend_sem, xrecv_sem) = scratch[2 * NB:]
     norb, bx = orb_hbm.shape[1], orb_hbm.shape[2]
     io, ix, iy = lax.axis_index("orb"), lax.axis_index("gx"), lax.axis_index("gyz")
     rows = pl.ds(ROW, 8)
@@ -135,7 +135,7 @@
         a, b = exists[dx][0], exists[dy][1]
         return b if a is None else a if b is None else jnp.logical_and(a, b)
 
-    sides = ((1, 0), (-1, 0), (0, 1), (0, -1), (1, 1), (1, -1), (-1, 1), (-1, -1))
+    sides = ((1, 1), (1, -1), (-1, 1), (-1, -1), (1, 0), (-1, 0), (0, 1), (0, -1))
 
     def span(d, length, first, width):
         if d == 0:
@@ -144,17 +144,31 @@
             return pl.ds(first + length - width, width), pl.ds(first - width, width)
         return pl.ds(first, width), pl.ds(first + length, width)
 
+    def inside(dx, dy):
+        ok = None
+        for d, at, n in ((dx, ix, nx), (dy, iy, ny)):
+            if d:
+                here = at < n - d if d > 0 else at >= -d
+                ok = here if ok is None else jnp.logical_and(ok, here)
+        return ok
+
+    def greet(sem, offsets):
+        for dx, dy in offsets:
+            @pl.when(inside(dx, dy))
+            def _():
+                pl.semaphore_signal(sem, inc=1, device_id=(io, ix + dx, iy + dy), device_id_type=MESH)
+
+    def await_greetings(sem, offsets):
+        pl.semaphore_wait(sem, sum(inside(dx, dy).astype(jnp.int32) for dx, dy in offsets))
+
+    def around(dx, dy):
+        return [(dx, 0), (-dx, 0), (0, dy), (0, -dy)]
+
+    first = list(sides) + [(0, 2), (0, -2)]
+    rounds = (around(1, 1) + [(0, 2), (0, -2)], around(2, 4), around(4, 8))
+    assert nx <= 8 and ny <= 16
     barrier = pltpu.get_barrier_semaphore()
-    for d in range(1, ny):
-        pl.semaphore_signal(barrier, inc=1, device_id=(io, ix, lax.rem(iy + d, ny)), device_id_type=MESH)
-    for d in range(1, nx):
-        pl.semaphore_signal(barrier, inc=1, device_id=(io, lax.rem(ix + d, nx), iy), device_id_type=MESH)
-    expected = nx + ny - 2
-    for dx, dy in sides[4:]:
-        @pl.when(present(dx, dy))
-        def _():
-            pl.semaphore_signal(barrier, inc=1, device_id=(io, ix + dx, iy + dy), device_id_type=MESH)
-        expected = expected + present(dx, dy).astype(jnp.int32)
+    greet(barrier, first)
 
     def pot_halo(side):
         dx, dy = sides[side]
@@ -213,10 +227,11 @@
 
     for copy in loads:
         copy.wait()
-    pl.semaphore_wait(barrier, expected)
+    await_greetings(barrier, first)
     each_side(True, lambda side: pot_halo(side).start())
     for o in range(norb):
         send(0, o)
+    greet(ready.at[0], rounds[0])
 
     zero, one = jnp.float32(0.0), jnp.float32(1.0)
     row = lax.broadcasted_iota(jnp.int32, (8, 128), 0)
@@ -324,7 +339,10 @@
                 column_products(g, o)
             return carry
         lax.fori_loop(0, norb, orbital, 0)
+        await_greetings(ready.at[g], rounds[g])
         if g < groups - 1:
+            greet(ready.at[g + 1], rounds[g + 1])
+
             def gram_columns(o, carry):
                 column_products(g, o)
                 return carry
@@ -432,6 +450,7 @@
                 pltpu.VMEM((ny, 8, 128), jnp.float32),
                 pltpu.VMEM((nx, 8, 128), jnp.float32),
                 pltpu.VMEM((2, NB, 2, 8, 128), jnp.float32),
+                pltpu.SemaphoreType.REGULAR((NB // GROUP,)),
                 pltpu.SemaphoreType.DMA((2 * norb + 1,)),
                 pltpu.SemaphoreType.DMA((2, 8)),
                 pltpu.SemaphoreType.DMA((NB // GROUP, norb, 8)),

time: 53.5 us -> 51.2 us (0.957)
  Pallas kernels: 49.1 us -> 46.8 us
    pallas_call x1, Pallas kernels: 49.1 us -> 46.8 us  [shards(): pl.pallas_call(functools.partial(kernel, nx, ny), out_shape=(block, block...]
where the time goes in v3:
time: 51.2 us; the launch traced here: 50.8 us
  Pallas kernels  46.8 us (91%)
  local copies, waits for them, and re-layouts  3.32 us (6%)
  between operations  0.65 us (1%)
    pallas_call x1, Pallas kernels, shards(): pl.pallas_call(functools.partial(kernel, nx, ny), out_shape=(block, block...  46.8 us
    unnamed x6, local copies, waits for them, and re-layouts  3.32 us

profile of v3, /device:TPU:6, one launch (start us, length us, event | category | flops | bytes accessed | tf_op | source)
XLA Modules:
  0.0 50.8 jit_solution(12111744379802716880)
XLA Ops:
  0.6 0.0 copy-start
  0.6 1.0 %copy-done = f32[2,3,16,8,128]{4,3,2,1,0:T(8,128)S(1)} copy-done((f32[2,3,16,8,128]{4,3,2,1,0:T(8,128)S(1)}, f32[2,3,16,8,128]{4,3,2,1,0:T(8,128)}, u32[]{:S(2)}) %copy-start) | copy-done | bytes 393240
  1.6 0.0 copy-start.1
  1.6 0.8 %copy-done.1 = f32[16,8,128]{2,1,0:T(8,128)S(1)} copy-done((f32[16,8,128]{2,1,0:T(8,128)S(1)}, f32[16,8,128]{2,1,0:T(8,128)}, u32[]{:S(2)}) %copy-start.1) | copy-done | bytes 65560
  2.5 46.8 %shard_map.41 = (f32[2,3,16,8,128]{4,3,2,1,0:T(8,128)S(1)}, f32[2,3,16,8,128]{4,3,2,1,0:T(8,128)S(1)}) custom-call(f32[2,3,16,8,128]{4,3,2,1,0:T(8,128)S(1)} %copy-done, f32[16,8,128]{2,1,0:T(8,128)S(1)} %copy-done.1), custom_call_target="tpu_custom_call" | custom-call | tf_op jit(solution)/shard_map/pallas_call | solution.py:435
  49.3 0.7 %copy.6 = f32[2,3,16,8,128]{4,3,2,1,0:T(8,128)} copy(f32[2,3,16,8,128]{4,3,2,1,0:T(8,128)S(1)} %get-tuple-element.4) | data formatting | bytes 786432
  50.0 0.7 %copy.7 = f32[2,3,16,8,128]{4,3,2,1,0:T(8,128)} copy(f32[2,3,16,8,128]{4,3,2,1,0:T(8,128)S(1)} %get-tuple-element.5) | data formatting | bytes 786432
Async XLA Ops:
  0.6 1.0 %copy-start = (f32[2,3,16,8,128]{4,3,2,1,0:T(8,128)S(1)}, f32[2,3,16,8,128]{4,3,2,1,0:T(8,128)}, u32[]{:S(2)}) copy-start(f32[2,3,16,8,128]{4,3,2,1,0:T(8,128)} %orb_hbm.1) | copy-start | bytes 1179652
  1.6 0.8 %copy-start.1 = (f32[16,8,128]{2,1,0:T(8,128)S(1)}, f32[16,8,128]{2,1,0:T(8,128)}, u32[]{:S(2)}) copy-start(f32[16,8,128]{2,1,0:T(8,128)} %pot_hbm.1) | copy-start | bytes 196612

commit v4 on v3

--- a/solution.py
+++ b/solution.py
@@ -114,9 +114,9 @@
 def kernel(
     nx, ny, orb_hbm, pot_hbm, evolved_ref, residual_ref, *scratch,
 ):
-    us, ws = scratch[:NB], scratch[NB:2 * NB]
-    (pot, pr, pi, qf, gram, part_y, part_x, coef,
-     ready, load_sem, pot_sem, send_sem, recv_sem, ysend_sem, yrecv_sem, xsend_sem, xrecv_sem) = scratch[2 * NB:]
+    us = scratch[:NB + 1]
+    (pot, pr, pi, qf, weight, gram, part_y, part_x,
+     ready, load_sem, pot_sem, send_sem, recv_sem, ysend_sem, yrecv_sem, xsend_sem, xrecv_sem) = scratch[NB + 1:]
     norb, bx = orb_hbm.shape[1], orb_hbm.shape[2]
     io, ix, iy = lax.axis_index("orb"), lax.axis_index("gx"), lax.axis_index("gyz")
     rows = pl.ds(ROW, 8)
@@ -249,6 +249,14 @@
             pr[x, tile] = p
             pi[x, tile] = -q * p
 
+    def weights(x, carry):
+        q = HALF_STEP * (DIAG + pot[x + NEAR, rows])
+        weight[x] = (1.0 + q * q) * (1.0 / KAPPA**2)
+        return carry
+
+    lax.fori_loop(0, bx, weights, 0, unroll=4)
+    await_greetings(ready.at[0], rounds[0])
+    greet(ready.at[1], rounds[1])
     each_side(False, lambda side: pot_halo(side).wait_recv())
     lax.fori_loop(0, NEAR, lambda x, c: (coefficients(x, jnp.where(low_x, one, zero)), c)[1], 0)
     lax.fori_loop(NEAR, bx + NEAR, lambda x, c: (coefficients(x, one), c)[1], 0, unroll=4)
@@ -268,12 +276,8 @@
         z2 = far[0] * pltpu.roll(center, 2, 1) + far[1] * pltpu.roll(center, 126, 1)
         return center, (s1 + z1) + (FAR * s2 + z2)
 
-    def wrows(s):
-        return pl.ds(ROW - RC, 8) if s % GROUP < GROUP - 1 else pl.ds(0, 8)
-
     def advance(s, o):
         u, margin = us[s], WIDTH - 2 - 2 * (s % GROUP)
-        a_shift, b_shift = SHIFT[s][0] / KAPPA, SHIFT[s][1] / KAPPA
         for x in range(-margin, bx + margin):
             out = -x if x < 0 else x - bx + 1 if x >= bx else 0
             beyond = margin - 2 * ((out + 1) // 2)
@@ -281,36 +285,31 @@
                 u_re, t_re = stencil(u, o, x, 0, r)
                 u_im, t_im = stencil(u, o, x, 1, r)
                 tile = pl.ds(r - RC, 8)
+                a, b = pr[x + NEAR, tile], pi[x + NEAR, tile]
                 if s == 0:
                     q = qf[x + NEAR, tile]
                     w_re = 2.0 * (KAPPA * t_im + q * u_im)
                     w_im = -2.0 * (KAPPA * t_re + q * u_re)
-                elif a_shift == 0.0:
-                    w_re, w_im = -t_im, t_re
+                    v_re, v_im = a * w_re - b * w_im, a * w_im + b * w_re
                 else:
-                    q = qf[x + NEAR, tile]
-                    a, b = a_shift - b_shift * q, b_shift + a_shift * q
-                    w_re = b * u_im - (t_im + a * u_re)
-                    w_im = t_re - (a * u_im + b * u_re)
-                if 0 <= x < bx:
-                    dest = pl.ds(r - RC, 8) if beyond else pl.ds(0, 8)
-                    ws[s][o, x, 0, dest] = w_re
-                    ws[s][o, x, 1, dest] = w_im
-                if s < NB - 1:
-                    a, b = pr[x + NEAR, tile], pi[x + NEAR, tile]
-                    us[s + 1][o, x + WIDTH, 0, pl.ds(r, 8)] = a * w_re - b * w_im
-                    us[s + 1][o, x + WIDTH, 1, pl.ds(r, 8)] = a * w_im + b * w_re
-
-    def vector(s, o, x):
-        return ws[s][o, x, 0, wrows(s)], ws[s][o, x, 1, wrows(s)]
+                    re, im = SHIFT[s]
+                    v_re, v_im = -(a * t_im + b * t_re), a * t_re - b * t_im
+                    if re != 0.0:
+                        v_re = (im * u_im - a * t_im) - (re * u_re + b * t_re)
+                        v_im = (a * t_re - re * u_im) - (im * u_re + b * t_im)
+                us[s + 1][o, x + WIDTH, 0, pl.ds(r, 8)] = v_re
+                us[s + 1][o, x + WIDTH, 1, pl.ds(r, 8)] = v_im
+
+    def vector(k, o, x):
+        return us[k + 1][o, x + WIDTH, 0, rows], us[k + 1][o, x + WIDTH, 1, rows]
 
     def products(o, pairs):
         acc = {}
-        used = sorted({k for pair in pairs for k in pair})
         for x in range(bx):
-            v = {k: vector(k, o, x) for k in used}
+            v = {k: vector(k, o, x) for k in sorted({k for pair in pairs for k in pair})}
+            weighted = {i: (weight[x] * v[i][0], weight[x] * v[i][1]) for i in sorted({i for i, _ in pairs})}
             for i, j in pairs:
-                (ar, ai), (br, bi) = v[i], v[j]
+                (ar, ai), (br, bi) = weighted[i], v[j]
                 terms = [ar * br + ai * bi] + ([ar * bi - ai * br] if i != j else [])
                 for part, term in enumerate(terms):
                     key = (i, j, part, x % 2)
@@ -326,6 +325,47 @@
             products(o, [(i, j) for j in new])
         products(o, [(i, j) for i in new for j in new if i <= j][:3])
         products(o, [(i, j) for i in new for j in new if i <= j][3:])
+
+    def exchange(part, o, me, n, target, ssem, rsem):
+        def copy(d, slot):
+            return pltpu.make_async_remote_copy(
+                src_ref=part.at[o, me], dst_ref=part.at[o, slot],
+                send_sem=ssem.at[o, d], recv_sem=rsem.at[o, slot],
+                device_id=target(lax.rem(me + d, n)), device_id_type=MESH,
+            )
+        order = sorted(range(1, n), key=lambda d: -min(d, n - d))
+
+        def start(row):
+            part[o, me] = row
+            for d in order:
+                copy(d, me).start()
+
+        def total():
+            for d in reversed(order):
+                copy(d, lax.rem(me + d, n)).wait_recv()
+            terms = [part[o, k] for k in range(n)]
+            while len(terms) > 1:
+                terms = [terms[k] + terms[k + 1] for k in range(0, len(terms), 2)]
+            return terms[0]
+
+        def drain():
+            for d in order:
+                copy(d, me).wait_send()
+
+        return start, total, drain
+
+    def over_y(o):
+        return exchange(part_y, o, iy, ny, lambda t: (io, ix, t), ysend_sem, yrecv_sem)
+
+    def over_x(o):
+        return exchange(part_x, o, ix, nx, lambda t: (io, t, iy), xsend_sem, xrecv_sem)
+
+    def start_reduction(o):
+        sums = lax.dot_general(
+            jnp.ones((8, 128), jnp.float32), gram[o], (((1,), (1,)), ((), ())),
+            precision=lax.Precision.HIGHEST, preferred_element_type=jnp.float32,
+        )
+        over_y(o)[0](sums[0:1])
 
     groups = NB // GROUP
     for g in range(groups):
@@ -337,86 +377,25 @@
                 send(g + 1, o)
             else:
                 column_products(g, o)
+                start_reduction(o)
             return carry
         lax.fori_loop(0, norb, orbital, 0)
-        await_greetings(ready.at[g], rounds[g])
+        if g == 0:
+            await_greetings(ready.at[1], rounds[1])
+            greet(ready.at[2], rounds[2])
+        if g == 1:
+            await_greetings(ready.at[2], rounds[2])
         if g < groups - 1:
-            greet(ready.at[g + 1], rounds[g + 1])
-
             def gram_columns(o, carry):
                 column_products(g, o)
                 return carry
             lax.fori_loop(0, norb, gram_columns, 0)
 
-    ones = jnp.ones((8, 128), jnp.float32)
-    mine = jnp.zeros((8, 128), jnp.float32)
-    for o in range(norb):
-        total = lax.dot_general(
-            ones, gram[o], (((1,), (1,)), ((), ())),
-            precision=lax.Precision.HIGHEST, preferred_element_type=jnp.float32,
-        )
-        mine = jnp.where(row == o, total, mine)
-
-    def gather(part, me, n, target, ssem, rsem):
-        def copy(d, slot):
-            return pltpu.make_async_remote_copy(
-                src_ref=part.at[me], dst_ref=part.at[slot],
-                send_sem=ssem.at[d], recv_sem=rsem.at[slot],
-                device_id=target(lax.rem(me + d, n)), device_id_type=MESH,
-            )
-        for d in range(1, n):
-            copy(d, me).start()
-        for d in range(1, n):
-            copy(d, lax.rem(me + d, n)).wait_recv()
-        for d in range(1, n):
-            copy(d, me).wait_send()
-        terms = [part[k] for k in range(n)]
-        while len(terms) > 1:
-            terms = [terms[k] + terms[k + 1] for k in range(0, len(terms), 2)]
-        return terms[0]
-
-    part_y[iy] = mine
-    line = gather(part_y, iy, ny, lambda t: (io, ix, t), ysend_sem, yrecv_sem)
-    part_x[ix] = line
-    total = gather(part_x, ix, nx, lambda t: (io, t, iy), xsend_sem, xrecv_sem)
-
-    def spread(e):
-        return jnp.broadcast_to(total[:, e:e + 1], (8, 128))
-
-    entries = {}
-    for j in range(NB):
-        for i in range(j + 1):
-            re = spread(tri(i, j))
-            im = jnp.zeros_like(re) if i == j else spread(IM + tri(i, j))
-            entries[i, j] = (re, im)
-            if i != j:
-                entries[j, i] = (re, -im)
-    res_coef, x_coef = recurrences(lambda i, j: entries[i, j])
-    for k in range(NB):
-        coef[0, k, 0], coef[0, k, 1] = res_coef[k]
-        if k < NB - 1:
-            coef[1, k, 0] = x_coef[k][0] * (1.0 / KAPPA)
-            coef[1, k, 1] = x_coef[k][1] * (1.0 / KAPPA)
-
-    for o in range(norb):
-        def take(kind, k, c):
-            return jnp.broadcast_to(coef[kind, k, c, pl.ds(o, 1)], (8, 128))
-
-        rc = [(take(0, k, 0), take(0, k, 1)) for k in range(NB)]
-        xc = [(take(1, k, 0), take(1, k, 1)) for k in range(NB - 1)]
-
-        def combine(x, carry):
-            vectors = [vector(k, o, x) for k in range(NB)]
-            res = csum([cmul(rc[k], vectors[k]) for k in range(NB)])
-            inc = csum([cmul(xc[k], vectors[k]) for k in range(NB - 1)])
-            inside = pl.ds(ROW - RC, 8)
-            inc = cmul((pr[x + NEAR, inside], pi[x + NEAR, inside]), inc)
-            for c in range(2):
-                residual_ref[c, o, x] = res[c]
-                evolved_ref[c, o, x] = us[0][o, x + WIDTH, c, rows] + inc[c]
-            return carry
-
-        lax.fori_loop(0, bx, combine, 0)
+    def second_stage(o, carry):
+        over_x(o)[0](over_y(o)[1]())
+        return carry
+
+    lax.fori_loop(0, norb, second_stage, 0)
 
     each_side(True, lambda side: pot_halo(side).wait_send())
     for g in range(groups):
@@ -424,6 +403,47 @@
             each_side(True, lambda side: halo(g, o, side).wait_send())
             return carry
         lax.fori_loop(0, norb, drain, 0)
+
+    def drain_first(o, carry):
+        over_y(o)[2]()
+        return carry
+
+    lax.fori_loop(0, norb, drain_first, 0)
+
+    def finish(o, carry):
+        total = jnp.broadcast_to(over_x(o)[1](), (8, 128))
+
+        def spread(e):
+            return jnp.broadcast_to(total[:, e:e + 1], (8, 128))
+
+        entries = {}
+        for j in range(NB):
+            for i in range(j + 1):
+                re = spread(tri(i, j))
+                im = jnp.zeros_like(re) if i == j else spread(IM + tri(i, j))
+                entries[i, j] = (re, im)
+                if i != j:
+                    entries[j, i] = (re, -im)
+        res_coef, x_coef = recurrences(lambda i, j: entries[i, j])
+        rc = [(c[0] * (1.0 / KAPPA), c[1] * (1.0 / KAPPA)) for c in res_coef]
+        xc = [(c[0] * (1.0 / KAPPA), c[1] * (1.0 / KAPPA)) for c in x_coef]
+
+        def combine(x, carry):
+            vectors = [vector(k, o, x) for k in range(NB)]
+            re, im = csum([cmul(rc[k], vectors[k]) for k in range(NB)])
+            inc = csum([cmul(xc[k], vectors[k]) for k in range(NB - 1)])
+            q = qf[x + NEAR, pl.ds(ROW - RC, 8)]
+            residual_ref[0, o, x] = re - q * im
+            residual_ref[1, o, x] = im + q * re
+            for c in range(2):
+                evolved_ref[c, o, x] = us[0][o, x + WIDTH, c, rows] + inc[c]
+            return carry
+
+        lax.fori_loop(0, bx, combine, 0, unroll=2)
+        over_x(o)[2]()
+        return carry
+
+    lax.fori_loop(0, norb, finish, 0)
 
 
 def solution(mesh):
@@ -438,32 +458,30 @@
             in_specs=[pl.BlockSpec(memory_space=pltpu.HBM)] * 2,
             out_specs=(pl.BlockSpec(memory_space=pltpu.VMEM), pl.BlockSpec(memory_space=pltpu.VMEM)),
             scratch_shapes=[
-                pltpu.VMEM((norb, bx + 2 * WIDTH, 2, by + 16, nz), jnp.float32) for _ in range(NB)
-            ] + [
-                pltpu.VMEM((norb, bx, 2, 16 if s % GROUP < GROUP - 1 else 8, nz), jnp.float32) for s in range(NB)
+                pltpu.VMEM((norb, bx + 2 * WIDTH, 2, by + 16, nz), jnp.float32) for _ in range(NB + 1)
             ] + [
                 pltpu.VMEM((bx + 2 * NEAR, by + 16, nz), jnp.float32),
                 pltpu.VMEM((bx + 2 * NEAR, 16, nz), jnp.float32),
                 pltpu.VMEM((bx + 2 * NEAR, 16, nz), jnp.float32),
                 pltpu.VMEM((bx + 2 * NEAR, 16, nz), jnp.float32),
+                pltpu.VMEM((bx, by, nz), jnp.float32),
                 pltpu.VMEM((norb, 128, 128), jnp.float32),
-                pltpu.VMEM((ny, 8, 128), jnp.float32),
-                pltpu.VMEM((nx, 8, 128), jnp.float32),
-                pltpu.VMEM((2, NB, 2, 8, 128), jnp.float32),
+                pltpu.VMEM((norb, ny, 1, 128), jnp.float32),
+                pltpu.VMEM((norb, nx, 1, 128), jnp.float32),
                 pltpu.SemaphoreType.REGULAR((NB // GROUP,)),
                 pltpu.SemaphoreType.DMA((2 * norb + 1,)),
                 pltpu.SemaphoreType.DMA((2, 8)),
                 pltpu.SemaphoreType.DMA((NB // GROUP, norb, 8)),
                 pltpu.SemaphoreType.DMA((NB // GROUP, norb, 8)),
-                pltpu.SemaphoreType.DMA((ny,)),
-                pltpu.SemaphoreType.DMA((ny,)),
-                pltpu.SemaphoreType.DMA((nx,)),
-                pltpu.SemaphoreType.DMA((nx,)),
+                pltpu.SemaphoreType.DMA((norb, ny)),
+                pltpu.SemaphoreType.DMA((norb, ny)),
+                pltpu.SemaphoreType.DMA((norb, nx)),
+                pltpu.SemaphoreType.DMA((norb, nx)),
             ],
             compiler_params=pltpu.CompilerParams(
                 collective_id=0, has_side_effects=True, vmem_limit_bytes=48 * 2**20
             ),
-        )(orbitals, potential)
+        )(*(pltpu.with_memory_space_constraint(a, pltpu.HBM) for a in (orbitals, potential)))
 
     spec = P(None, "orb", "gx", "gyz", None)
     return jax.shard_map(

time: 51.2 us -> 47.9 us (0.936)
  local copies, waits for them, and re-layouts: 3.32 us -> 1.49 us
  Pallas kernels: 46.8 us -> 45.6 us
    unnamed x6 -> x2, local copies, waits for them, and re-layouts: 3.32 us -> 1.49 us
    pallas_call x1, Pallas kernels: 46.8 us -> 45.6 us  [shards(): pl.pallas_call(functools.partial(kernel, nx, ny), out_shape=(block, block...]
where the time goes in v4:
time: 47.9 us; the launch traced here: 47.7 us
  Pallas kernels  45.6 us (95%)
  local copies, waits for them, and re-layouts  1.49 us (3%)
  between operations  0.64 us (1%)
    pallas_call x1, Pallas kernels, shards(): pl.pallas_call(functools.partial(kernel, nx, ny), out_shape=(block, block...  45.6 us
    unnamed x2, local copies, waits for them, and re-layouts  1.49 us

profile of v4, /device:TPU:6, one launch (start us, length us, event | category | flops | bytes accessed | tf_op | source)
XLA Modules:
  0.0 47.7 jit_solution(5657827089809784341)
XLA Ops:
  0.6 45.6 %shard_map.41 = (f32[2,3,16,8,128]{4,3,2,1,0:T(8,128)S(1)}, f32[2,3,16,8,128]{4,3,2,1,0:T(8,128)S(1)}) custom-call(f32[2,3,16,8,128]{4,3,2,1,0:T(8,128)} %orb_hbm.1, f32[16,8,128]{2,1,0:T(8,128)} %pot_hbm.1), custom_call_target="tpu_custom_call" | custom-call | tf_op jit(solution)/shard_map/pallas_call | solution.py:455
  46.2 0.7 %copy.6 = f32[2,3,16,8,128]{4,3,2,1,0:T(8,128)} copy(f32[2,3,16,8,128]{4,3,2,1,0:T(8,128)S(1)} %get-tuple-element.4) | data formatting | bytes 786432
  47.0 0.7 %copy.7 = f32[2,3,16,8,128]{4,3,2,1,0:T(8,128)} copy(f32[2,3,16,8,128]{4,3,2,1,0:T(8,128)S(1)} %get-tuple-element.5) | data formatting | bytes 786432

commit v5 on v4

--- a/solution.py
+++ b/solution.py
@@ -114,19 +114,21 @@
 def kernel(
     nx, ny, orb_hbm, pot_hbm, evolved_ref, residual_ref, *scratch,
 ):
-    us = scratch[:NB + 1]
-    (pot, pr, pi, qf, weight, gram, part_y, part_x,
-     ready, load_sem, pot_sem, send_sem, recv_sem, ysend_sem, yrecv_sem, xsend_sem, xrecv_sem) = scratch[NB + 1:]
+    (ux, *us) = scratch[:NB + 2 - NB // GROUP]
+    us = [ux.at[k // GROUP] if k % GROUP == 0 and k < NB else us.pop(0) for k in range(NB + 1)]
+    (pot, ballast, pr, pi, qf, weight, gram, part_y, part_x,
+     ready, load_sem, pot_sem, send_sem, recv_sem, ysend_sem, yrecv_sem, xsend_sem, xrecv_sem) = scratch[NB + 2 - NB // GROUP:]
     norb, bx = orb_hbm.shape[1], orb_hbm.shape[2]
     io, ix, iy = lax.axis_index("orb"), lax.axis_index("gx"), lax.axis_index("gyz")
     rows = pl.ds(ROW, 8)
 
-    loads = [pltpu.make_async_copy(pot_hbm, pot.at[pl.ds(NEAR, bx), rows], load_sem.at[2 * norb])] + [
-        pltpu.make_async_copy(orb_hbm.at[c, o], us[0].at[o, pl.ds(WIDTH, bx), c, rows], load_sem.at[2 * o + c])
-        for o in range(norb) for c in range(2)
-    ]
-    for copy in loads:
-        copy.start()
+    load_pot = pltpu.make_async_copy(pot_hbm, pot.at[pl.ds(NEAR, bx), rows], load_sem.at[0])
+    load_pot.start()
+    for o in range(norb):
+        for c in range(2):
+            pltpu.make_async_copy(
+                orb_hbm.at[c, o], us[0].at[o, pl.ds(WIDTH, bx), c, rows], load_sem.at[1]
+            ).start()
 
     low_x, high_x, low_y, high_y = ix > 0, ix < nx - 1, iy > 0, iy < ny - 1
     exists = {-1: (low_x, low_y), 0: (None, None), 1: (high_x, high_y)}
@@ -175,32 +177,50 @@
         (sx, tx), (sr, tr) = span(dx, bx, NEAR, NEAR), span(dy, 8, ROW, NEAR)
         return pltpu.make_async_remote_copy(
             src_ref=pot.at[sx, sr], dst_ref=pot.at[tx, tr],
-            send_sem=pot_sem.at[0, side], recv_sem=pot_sem.at[1, side],
+            send_sem=pot_sem.at[0], recv_sem=pot_sem.at[1],
             device_id=(io, ix + dx, iy + dy), device_id_type=MESH,
         )
 
+    def halo_spans(side):
+        dx, dy = sides[side]
+        width = NEAR if dx and dy else WIDTH
+        return span(dx, bx, WIDTH, width), span(dy, 8, ROW, width)
+
     def halo(g, o, side):
         dx, dy = sides[side]
-        width = NEAR if dx and dy else WIDTH
-        (sx, tx), (sr, tr) = span(dx, bx, WIDTH, width), span(dy, 8, ROW, width)
+        (sx, tx), (sr, tr) = halo_spans(side)
         ref = us[GROUP * g]
         return pltpu.make_async_remote_copy(
             src_ref=ref.at[o, sx, :, sr], dst_ref=ref.at[o, tx, :, tr],
-            send_sem=send_sem.at[g, o, side], recv_sem=recv_sem.at[g, o, side],
+            send_sem=send_sem.at[side], recv_sem=recv_sem.at[g % 2, o],
             device_id=(io, ix + dx, iy + dy), device_id_type=MESH,
         )
 
-    def each_side(sent, act):
+    def each_side(act):
         for side, (dx, dy) in enumerate(sides):
-            @pl.when(present(dx, dy) if sent else present(-dx, -dy))
+            @pl.when(present(dx, dy))
             def _():
                 act(side)
 
     def send(g, o):
-        each_side(True, lambda side: halo(g, o, side).start())
+        each_side(lambda side: halo(g, o, side).start())
+
+    both_x, both_y = jnp.logical_and(low_x, high_x), jnp.logical_and(low_y, high_y)
+
+    def await_sides(sem, planes, wide, corner):
+        for nsx in (1, 2):
+            for nsy in (1, 2):
+                here = jnp.logical_and(both_x if nsx == 2 else jnp.logical_not(both_x),
+                                       both_y if nsy == 2 else jnp.logical_not(both_y))
+                total = planes * (nsx * wide * 8 + nsy * bx * wide + nsx * nsy * corner * corner)
+                ref = ballast.at[pl.ds(0, total)]
+
+                @pl.when(here)
+                def _():
+                    pltpu.make_async_copy(ref, ref, sem).wait()
 
     def receive(g, o):
-        each_side(False, lambda side: halo(g, o, side).wait_recv())
+        await_sides(recv_sem.at[g % 2, o], 2, WIDTH, NEAR)
 
     def clear(x0, nplanes, r0, nrows):
         def body(x, carry):
@@ -225,10 +245,11 @@
             clear_pot(0, bx + 2 * NEAR, ROW - NEAR if r0 < ROW else ROW + 8, NEAR)
     gram[...] = jnp.zeros_like(gram)
 
-    for copy in loads:
-        copy.wait()
+    block = us[0].at[:, pl.ds(WIDTH, bx), :, rows]
+    load_pot.wait()
+    pltpu.make_async_copy(block, block, load_sem.at[1]).wait()
     await_greetings(barrier, first)
-    each_side(True, lambda side: pot_halo(side).start())
+    each_side(lambda side: pot_halo(side).start())
     for o in range(norb):
         send(0, o)
     greet(ready.at[0], rounds[0])
@@ -257,7 +278,7 @@
     lax.fori_loop(0, bx, weights, 0, unroll=4)
     await_greetings(ready.at[0], rounds[0])
     greet(ready.at[1], rounds[1])
-    each_side(False, lambda side: pot_halo(side).wait_recv())
+    await_sides(pot_sem.at[1], 1, NEAR, NEAR)
     lax.fori_loop(0, NEAR, lambda x, c: (coefficients(x, jnp.where(low_x, one, zero)), c)[1], 0)
     lax.fori_loop(NEAR, bx + NEAR, lambda x, c: (coefficients(x, one), c)[1], 0, unroll=4)
     lax.fori_loop(bx + NEAR, bx + 2 * NEAR, lambda x, c: (coefficients(x, jnp.where(high_x, one, zero)), c)[1], 0)
@@ -326,46 +347,38 @@
         products(o, [(i, j) for i in new for j in new if i <= j][:3])
         products(o, [(i, j) for i in new for j in new if i <= j][3:])
 
-    def exchange(part, o, me, n, target, ssem, rsem):
-        def copy(d, slot):
-            return pltpu.make_async_remote_copy(
-                src_ref=part.at[o, me], dst_ref=part.at[o, slot],
-                send_sem=ssem.at[o, d], recv_sem=rsem.at[o, slot],
-                device_id=target(lax.rem(me + d, n)), device_id_type=MESH,
-            )
-        order = sorted(range(1, n), key=lambda d: -min(d, n - d))
-
-        def start(row):
+    def exchange(part, me, n, target, ssem, rsem):
+        def start(o, row):
             part[o, me] = row
-            for d in order:
-                copy(d, me).start()
-
-        def total():
-            for d in reversed(order):
-                copy(d, lax.rem(me + d, n)).wait_recv()
+            for d in sorted(range(1, n), key=lambda d: -min(d, n - d)):
+                pltpu.make_async_remote_copy(
+                    src_ref=part.at[o, me], dst_ref=part.at[o, me], send_sem=ssem, recv_sem=rsem.at[o],
+                    device_id=target(lax.rem(me + d, n)), device_id_type=MESH,
+                ).start()
+
+        def total(o):
+            others = part.at[o, pl.ds(0, n - 1)]
+            pltpu.make_async_copy(others, others, rsem.at[o]).wait()
             terms = [part[o, k] for k in range(n)]
             while len(terms) > 1:
                 terms = [terms[k] + terms[k + 1] for k in range(0, len(terms), 2)]
             return terms[0]
 
         def drain():
-            for d in order:
-                copy(d, me).wait_send()
+            others = part.at[:, pl.ds(0, n - 1)]
+            pltpu.make_async_copy(others, others, ssem).wait()
 
         return start, total, drain
 
-    def over_y(o):
-        return exchange(part_y, o, iy, ny, lambda t: (io, ix, t), ysend_sem, yrecv_sem)
-
-    def over_x(o):
-        return exchange(part_x, o, ix, nx, lambda t: (io, t, iy), xsend_sem, xrecv_sem)
+    start_y, total_y, drain_y = exchange(part_y, iy, ny, lambda t: (io, ix, t), ysend_sem.at[0], yrecv_sem)
+    start_x, total_x, drain_x = exchange(part_x, ix, nx, lambda t: (io, t, iy), xsend_sem.at[0], xrecv_sem)
 
     def start_reduction(o):
         sums = lax.dot_general(
             jnp.ones((8, 128), jnp.float32), gram[o], (((1,), (1,)), ((), ())),
             precision=lax.Precision.HIGHEST, preferred_element_type=jnp.float32,
         )
-        over_y(o)[0](sums[0:1])
+        start_y(o, sums[0:1])
 
     groups = NB // GROUP
     for g in range(groups):
@@ -392,26 +405,23 @@
             lax.fori_loop(0, norb, gram_columns, 0)
 
     def second_stage(o, carry):
-        over_x(o)[0](over_y(o)[1]())
+        start_x(o, total_y(o))
         return carry
 
     lax.fori_loop(0, norb, second_stage, 0)
 
-    each_side(True, lambda side: pot_halo(side).wait_send())
-    for g in range(groups):
-        def drain(o, carry):
-            each_side(True, lambda side: halo(g, o, side).wait_send())
-            return carry
-        lax.fori_loop(0, norb, drain, 0)
-
-    def drain_first(o, carry):
-        over_y(o)[2]()
-        return carry
-
-    lax.fori_loop(0, norb, drain_first, 0)
+    await_sides(pot_sem.at[0], 1, NEAR, NEAR)
+    for side, (dx, dy) in enumerate(sides):
+        (sx, _), (sr, _) = halo_spans(side)
+        sent = ux.at[:, :, sx, :, sr]
+
+        @pl.when(present(dx, dy))
+        def _():
+            pltpu.make_async_copy(sent, sent, send_sem.at[side]).wait()
+    drain_y()
 
     def finish(o, carry):
-        total = jnp.broadcast_to(over_x(o)[1](), (8, 128))
+        total = jnp.broadcast_to(total_x(o), (8, 128))
 
         def spread(e):
             return jnp.broadcast_to(total[:, e:e + 1], (8, 128))
@@ -440,10 +450,10 @@
             return carry
 
         lax.fori_loop(0, bx, combine, 0, unroll=2)
-        over_x(o)[2]()
         return carry
 
     lax.fori_loop(0, norb, finish, 0)
+    drain_x()
 
 
 def solution(mesh):
@@ -458,9 +468,12 @@
             in_specs=[pl.BlockSpec(memory_space=pltpu.HBM)] * 2,
             out_specs=(pl.BlockSpec(memory_space=pltpu.VMEM), pl.BlockSpec(memory_space=pltpu.VMEM)),
             scratch_shapes=[
-                pltpu.VMEM((norb, bx + 2 * WIDTH, 2, by + 16, nz), jnp.float32) for _ in range(NB + 1)
+                pltpu.VMEM((NB // GROUP, norb, bx + 2 * WIDTH, 2, by + 16, nz), jnp.float32)
+            ] + [
+                pltpu.VMEM((norb, bx + 2 * WIDTH, 2, by + 16, nz), jnp.float32) for _ in range(NB + 1 - NB // GROUP)
             ] + [
                 pltpu.VMEM((bx + 2 * NEAR, by + 16, nz), jnp.float32),
+                pltpu.VMEM((4 * (WIDTH * 8 + bx * WIDTH + 2 * NEAR * NEAR), nz), jnp.float32),
                 pltpu.VMEM((bx + 2 * NEAR, 16, nz), jnp.float32),
                 pltpu.VMEM((bx + 2 * NEAR, 16, nz), jnp.float32),
                 pltpu.VMEM((bx + 2 * NEAR, 16, nz), jnp.float32),
@@ -469,14 +482,14 @@
                 pltpu.VMEM((norb, ny, 1, 128), jnp.float32),
                 pltpu.VMEM((norb, nx, 1, 128), jnp.float32),
                 pltpu.SemaphoreType.REGULAR((NB // GROUP,)),
-                pltpu.SemaphoreType.DMA((2 * norb + 1,)),
-                pltpu.SemaphoreType.DMA((2, 8)),
-                pltpu.SemaphoreType.DMA((NB // GROUP, norb, 8)),
-                pltpu.SemaphoreType.DMA((NB // GROUP, norb, 8)),
-                pltpu.SemaphoreType.DMA((norb, ny)),
-                pltpu.SemaphoreType.DMA((norb, ny)),
-                pltpu.SemaphoreType.DMA((norb, nx)),
-                pltpu.SemaphoreType.DMA((norb, nx)),
+                pltpu.SemaphoreType.DMA((2,)),
+                pltpu.SemaphoreType.DMA((2,)),
+                pltpu.SemaphoreType.DMA((8,)),
+                pltpu.SemaphoreType.DMA((2, norb)),
+                pltpu.SemaphoreType.DMA((1,)),
+                pltpu.SemaphoreType.DMA((norb,)),
+                pltpu.SemaphoreType.DMA((1,)),
+                pltpu.SemaphoreType.DMA((norb,)),
             ],
             compiler_params=pltpu.CompilerParams(
                 collective_id=0, has_side_effects=True, vmem_limit_bytes=48 * 2**20

time: 47.9 us -> 45.3 us (0.946)
  Pallas kernels: 45.6 us -> 43 us
    pallas_call x1, Pallas kernels: 45.6 us -> 43 us  [shards(): pl.pallas_call(functools.partial(kernel, nx, ny), out_shape=(block, block...]
where the time goes in v5:
time: 45.3 us; the launch traced here: 45.2 us
  Pallas kernels  43 us (95%)
  local copies, waits for them, and re-layouts  1.49 us (3%)
  between operations  0.64 us (1%)
    pallas_call x1, Pallas kernels, shards(): pl.pallas_call(functools.partial(kernel, nx, ny), out_shape=(block, block...  43 us
    unnamed x2, local copies, waits for them, and re-layouts  1.49 us

profile of v5, /device:TPU:6, one launch (start us, length us, event | category | flops | bytes accessed | tf_op | source)
XLA Modules:
  0.0 45.2 jit_solution(11296836393357435381)
XLA Ops:
  0.6 43.0 %shard_map.41 = (f32[2,3,16,8,128]{4,3,2,1,0:T(8,128)S(1)}, f32[2,3,16,8,128]{4,3,2,1,0:T(8,128)S(1)}) custom-call(f32[2,3,16,8,128]{4,3,2,1,0:T(8,128)} %orb_hbm.1, f32[16,8,128]{2,1,0:T(8,128)} %pot_hbm.1), custom_call_target="tpu_custom_call" | custom-call | tf_op jit(solution)/shard_map/pallas_call | solution.py:465
  43.7 0.7 %copy.6 = f32[2,3,16,8,128]{4,3,2,1,0:T(8,128)} copy(f32[2,3,16,8,128]{4,3,2,1,0:T(8,128)S(1)} %get-tuple-element.4) | data formatting | bytes 786432
  44.4 0.7 %copy.7 = f32[2,3,16,8,128]{4,3,2,1,0:T(8,128)} copy(f32[2,3,16,8,128]{4,3,2,1,0:T(8,128)S(1)} %get-tuple-element.5) | data formatting | bytes 786432

commit v6 on v5

--- a/solution.py
+++ b/solution.py
@@ -112,11 +112,11 @@
 
 
 def kernel(
-    nx, ny, orb_hbm, pot_hbm, evolved_ref, residual_ref, *scratch,
+    nx, ny, orb_hbm, pot_hbm, out_ref, *scratch,
 ):
     (ux, *us) = scratch[:NB + 2 - NB // GROUP]
     us = [ux.at[k // GROUP] if k % GROUP == 0 and k < NB else us.pop(0) for k in range(NB + 1)]
-    (pot, ballast, pr, pi, qf, weight, gram, part_y, part_x,
+    (stage, pot, ballast, pr, pi, qf, weight, gram, part_y, part_x,
      ready, load_sem, pot_sem, send_sem, recv_sem, ysend_sem, yrecv_sem, xsend_sem, xrecv_sem) = scratch[NB + 2 - NB // GROUP:]
     norb, bx = orb_hbm.shape[1], orb_hbm.shape[2]
     io, ix, iy = lax.axis_index("orb"), lax.axis_index("gx"), lax.axis_index("gyz")
@@ -124,11 +124,8 @@
 
     load_pot = pltpu.make_async_copy(pot_hbm, pot.at[pl.ds(NEAR, bx), rows], load_sem.at[0])
     load_pot.start()
-    for o in range(norb):
-        for c in range(2):
-            pltpu.make_async_copy(
-                orb_hbm.at[c, o], us[0].at[o, pl.ds(WIDTH, bx), c, rows], load_sem.at[1]
-            ).start()
+    load_orb = pltpu.make_async_copy(orb_hbm, stage, load_sem.at[1])
+    load_orb.start()
 
     low_x, high_x, low_y, high_y = ix > 0, ix < nx - 1, iy > 0, iy < ny - 1
     exists = {-1: (low_x, low_y), 0: (None, None), 1: (high_x, high_y)}
@@ -174,7 +171,8 @@
 
     def pot_halo(side):
         dx, dy = sides[side]
-        (sx, tx), (sr, tr) = span(dx, bx, NEAR, NEAR), span(dy, 8, ROW, NEAR)
+        width = NEAR - 2 if dx and dy else NEAR
+        (sx, tx), (sr, tr) = span(dx, bx, NEAR, width), span(dy, 8, ROW, width)
         return pltpu.make_async_remote_copy(
             src_ref=pot.at[sx, sr], dst_ref=pot.at[tx, tr],
             send_sem=pot_sem.at[0], recv_sem=pot_sem.at[1],
@@ -183,18 +181,28 @@
 
     def halo_spans(side):
         dx, dy = sides[side]
-        width = NEAR if dx and dy else WIDTH
-        return span(dx, bx, WIDTH, width), span(dy, 8, ROW, width)
+        if not (dx and dy):
+            return [(span(dx, bx, WIDTH, WIDTH), span(dy, 8, ROW, WIDTH))]
+        pieces = []
+        for k in range(GROUP - 1):
+            from_x = span(dx, bx, WIDTH, 2)
+            from_x = tuple(pl.ds(at.start - 2 * k * dx, 2) for at in from_x)
+            pieces.append((from_x, span(dy, 8, ROW, NEAR - 2 * k)))
+        return pieces
 
     def halo(g, o, side):
         dx, dy = sides[side]
-        (sx, tx), (sr, tr) = halo_spans(side)
         ref = us[GROUP * g]
-        return pltpu.make_async_remote_copy(
-            src_ref=ref.at[o, sx, :, sr], dst_ref=ref.at[o, tx, :, tr],
-            send_sem=send_sem.at[side], recv_sem=recv_sem.at[g % 2, o],
-            device_id=(io, ix + dx, iy + dy), device_id_type=MESH,
-        )
+        return [
+            pltpu.make_async_remote_copy(
+                src_ref=ref.at[o, sx, :, sr], dst_ref=ref.at[o, tx, :, tr],
+                send_sem=send_sem.at[side], recv_sem=recv_sem.at[g % 2, o],
+                device_id=(io, ix + dx, iy + dy), device_id_type=MESH,
+            )
+            for (sx, tx), (sr, tr) in halo_spans(side)
+        ]
+
+    corner_cells = sum(2 * (NEAR - 2 * k) for k in range(GROUP - 1))
 
     def each_side(act):
         for side, (dx, dy) in enumerate(sides):
@@ -203,7 +211,7 @@
                 act(side)
 
     def send(g, o):
-        each_side(lambda side: halo(g, o, side).start())
+        each_side(lambda side: [copy.start() for copy in halo(g, o, side)])
 
     both_x, both_y = jnp.logical_and(low_x, high_x), jnp.logical_and(low_y, high_y)
 
@@ -212,7 +220,7 @@
             for nsy in (1, 2):
                 here = jnp.logical_and(both_x if nsx == 2 else jnp.logical_not(both_x),
                                        both_y if nsy == 2 else jnp.logical_not(both_y))
-                total = planes * (nsx * wide * 8 + nsy * bx * wide + nsx * nsy * corner * corner)
+                total = planes * (nsx * wide * 8 + nsy * bx * wide + nsx * nsy * corner)
                 ref = ballast.at[pl.ds(0, total)]
 
                 @pl.when(here)
@@ -220,7 +228,7 @@
                     pltpu.make_async_copy(ref, ref, sem).wait()
 
     def receive(g, o):
-        await_sides(recv_sem.at[g % 2, o], 2, WIDTH, NEAR)
+        await_sides(recv_sem.at[g % 2, o], 2, WIDTH, corner_cells)
 
     def clear(x0, nplanes, r0, nrows):
         def body(x, carry):
@@ -245,12 +253,20 @@
             clear_pot(0, bx + 2 * NEAR, ROW - NEAR if r0 < ROW else ROW + 8, NEAR)
     gram[...] = jnp.zeros_like(gram)
 
-    block = us[0].at[:, pl.ds(WIDTH, bx), :, rows]
     load_pot.wait()
-    pltpu.make_async_copy(block, block, load_sem.at[1]).wait()
+    load_orb.wait()
+
+    def unpack(o):
+        for x in range(bx):
+            for c in range(2):
+                us[0][o, x + WIDTH, c, rows] = stage[c, o, x]
+
+    unpack(0)
     await_greetings(barrier, first)
     each_side(lambda side: pot_halo(side).start())
-    for o in range(norb):
+    send(0, 0)
+    for o in range(1, norb):
+        unpack(o)
         send(0, o)
     greet(ready.at[0], rounds[0])
 
@@ -278,7 +294,7 @@
     lax.fori_loop(0, bx, weights, 0, unroll=4)
     await_greetings(ready.at[0], rounds[0])
     greet(ready.at[1], rounds[1])
-    await_sides(pot_sem.at[1], 1, NEAR, NEAR)
+    await_sides(pot_sem.at[1], 1, NEAR, (NEAR - 2) ** 2)
     lax.fori_loop(0, NEAR, lambda x, c: (coefficients(x, jnp.where(low_x, one, zero)), c)[1], 0)
     lax.fori_loop(NEAR, bx + NEAR, lambda x, c: (coefficients(x, one), c)[1], 0, unroll=4)
     lax.fori_loop(bx + NEAR, bx + 2 * NEAR, lambda x, c: (coefficients(x, jnp.where(high_x, one, zero)), c)[1], 0)
@@ -410,10 +426,10 @@
 
     lax.fori_loop(0, norb, second_stage, 0)
 
-    await_sides(pot_sem.at[0], 1, NEAR, NEAR)
+    await_sides(pot_sem.at[0], 1, NEAR, (NEAR - 2) ** 2)
     for side, (dx, dy) in enumerate(sides):
-        (sx, _), (sr, _) = halo_spans(side)
-        sent = ux.at[:, :, sx, :, sr]
+        cells = sum(sx.size * sr.size for (sx, _), (sr, _) in halo_spans(side))
+        sent = ux.at[:, :, pl.ds(0, cells // 4), :, pl.ds(ROW, 4)]
 
         @pl.when(present(dx, dy))
         def _():
@@ -443,13 +459,13 @@
             re, im = csum([cmul(rc[k], vectors[k]) for k in range(NB)])
             inc = csum([cmul(xc[k], vectors[k]) for k in range(NB - 1)])
             q = qf[x + NEAR, pl.ds(ROW - RC, 8)]
-            residual_ref[0, o, x] = re - q * im
-            residual_ref[1, o, x] = im + q * re
+            out_ref[1, 0, o, x] = re - q * im
+            out_ref[1, 1, o, x] = im + q * re
             for c in range(2):
-                evolved_ref[c, o, x] = us[0][o, x + WIDTH, c, rows] + inc[c]
+                out_ref[0, c, o, x] = stage[c, o, x] + inc[c]
             return carry
 
-        lax.fori_loop(0, bx, combine, 0, unroll=2)
+        lax.fori_loop(0, bx, combine, 0, unroll=4)
         return carry
 
     lax.fori_loop(0, norb, finish, 0)
@@ -461,17 +477,17 @@
 
     def shards(orbitals, potential):
         _, norb, bx, by, nz = orbitals.shape
-        block = jax.ShapeDtypeStruct(orbitals.shape, jnp.float32)
-        return pl.pallas_call(
+        both = pl.pallas_call(
             functools.partial(kernel, nx, ny),
-            out_shape=(block, block),
+            out_shape=jax.ShapeDtypeStruct((2, *orbitals.shape), jnp.float32),
             in_specs=[pl.BlockSpec(memory_space=pltpu.HBM)] * 2,
-            out_specs=(pl.BlockSpec(memory_space=pltpu.VMEM), pl.BlockSpec(memory_space=pltpu.VMEM)),
+            out_specs=pl.BlockSpec(memory_space=pltpu.VMEM),
             scratch_shapes=[
                 pltpu.VMEM((NB // GROUP, norb, bx + 2 * WIDTH, 2, by + 16, nz), jnp.float32)
             ] + [
                 pltpu.VMEM((norb, bx + 2 * WIDTH, 2, by + 16, nz), jnp.float32) for _ in range(NB + 1 - NB // GROUP)
             ] + [
+                pltpu.VMEM(orbitals.shape, jnp.float32),
                 pltpu.VMEM((bx + 2 * NEAR, by + 16, nz), jnp.float32),
                 pltpu.VMEM((4 * (WIDTH * 8 + bx * WIDTH + 2 * NEAR * NEAR), nz), jnp.float32),
                 pltpu.VMEM((bx + 2 * NEAR, 16, nz), jnp.float32),
@@ -495,6 +511,7 @@
                 collective_id=0, has_side_effects=True, vmem_limit_bytes=48 * 2**20
             ),
         )(*(pltpu.with_memory_space_constraint(a, pltpu.HBM) for a in (orbitals, potential)))
+        return both[0], both[1]
 
     spec = P(None, "orb", "gx", "gyz", None)
     return jax.shard_map(

time: 45.3 us -> 43.7 us (0.965)
  Pallas kernels: 43 us -> 42 us
  local copies, waits for them, and re-layouts: 1.49 us -> 0.93 us
    unnamed x2 -> x0, local copies, waits for them, and re-layouts: 1.49 us -> none
    pallas_call x1, Pallas kernels: 43 us -> 42 us  [shards(): pl.pallas_call(functools.partial(kernel, nx, ny), out_shape=jax.ShapeDtyp...]
    squeeze x0 -> x1, local copies, waits for them, and re-layouts: none -> 0.93 us  [shards(): return (both[0], both[1])]
where the time goes in v6:
time: 43.7 us; the launch traced here: 43.6 us
  Pallas kernels  42 us (96%)
  local copies, waits for them, and re-layouts  0.93 us (2%)
  between operations  0.64 us (1%)
    pallas_call x1, Pallas kernels, shards(): pl.pallas_call(functools.partial(kernel, nx, ny), out_shape=jax.ShapeDtyp...  42 us
    squeeze x1, local copies, waits for them, and re-layouts, shards(): return (both[0], both[1])  0.93 us

profile of v6, /device:TPU:6, one launch (start us, length us, event | category | flops | bytes accessed | tf_op | source)
XLA Modules:
  0.0 43.6 jit_solution(13519218843317277782)
XLA Ops:
  0.6 42.0 %shard_map.41 = f32[2,2,3,16,8,128]{5,4,3,2,1,0:T(8,128)S(1)} custom-call(f32[2,3,16,8,128]{4,3,2,1,0:T(8,128)} %orb_hbm.1, f32[16,8,128]{2,1,0:T(8,128)} %pot_hbm.1), custom_call_target="tpu_custom_call" | custom-call | tf_op jit(solution)/shard_map/pallas_call | solution.py:480
  42.7 0.9 %slice_bitcast_fusion = (f32[2,3,16,8,128]{4,3,2,1,0:T(8,128)}, f32[2,3,16,8,128]{4,3,2,1,0:T(8,128)}) fusion(f32[2,2,3,16,8,128]{5,4,3,2,1,0:T(8,128)S(1)} %shard_map.41), kind=kLoop, calls=%fused_computation | loop fusion | bytes 1572864 | tf_op jit(solution)/shard_map/squeeze | solution.py:514

commit v7 on v6

--- a/solution.py
+++ b/solution.py
@@ -174,7 +174,8 @@
         width = NEAR - 2 if dx and dy else NEAR
         (sx, tx), (sr, tr) = span(dx, bx, NEAR, width), span(dy, 8, ROW, width)
         return pltpu.make_async_remote_copy(
-            src_ref=pot.at[sx, sr], dst_ref=pot.at[tx, tr],
+            src_ref=pot_hbm.at[pl.ds(sx.start - NEAR, sx.size), pl.ds(sr.start - ROW, sr.size)],
+            dst_ref=pot.at[tx, tr],
             send_sem=pot_sem.at[0], recv_sem=pot_sem.at[1],
             device_id=(io, ix + dx, iy + dy), device_id_type=MESH,
         )
@@ -230,6 +231,9 @@
     def receive(g, o):
         await_sides(recv_sem.at[g % 2, o], 2, WIDTH, corner_cells)
 
+    await_greetings(barrier, first)
+    each_side(lambda side: pot_halo(side).start())
+
     def clear(x0, nplanes, r0, nrows):
         def body(x, carry):
             for g in range(NB // GROUP):
@@ -251,7 +255,6 @@
         def _():
             clear(0, bx + 2 * WIDTH, r0, WIDTH)
             clear_pot(0, bx + 2 * NEAR, ROW - NEAR if r0 < ROW else ROW + 8, NEAR)
-    gram[...] = jnp.zeros_like(gram)
 
     load_pot.wait()
     load_orb.wait()
@@ -262,8 +265,6 @@
                 us[0][o, x + WIDTH, c, rows] = stage[c, o, x]
 
     unpack(0)
-    await_greetings(barrier, first)
-    each_side(lambda side: pot_halo(side).start())
     send(0, 0)
     for o in range(1, norb):
         unpack(o)

time: 43.7 us -> 43.9 us (level)
  no operation moved by 1% of the time
where the time goes in v7:
time: 43.9 us; the launch traced here: 43.8 us
  Pallas kernels  42.2 us (96%)
  local copies, waits for them, and re-layouts  0.93 us (2%)
  between operations  0.64 us (1%)
    pallas_call x1, Pallas kernels, shards(): pl.pallas_call(functools.partial(kernel, nx, ny), out_shape=jax.ShapeDtyp...  42.2 us
    squeeze x1, local copies, waits for them, and re-layouts, shards(): return (both[0], both[1])  0.93 us

profile of v7, /device:TPU:6, one launch (start us, length us, event | category | flops | bytes accessed | tf_op | source)
XLA Modules:
  0.0 43.8 jit_solution(9019907472923436991)
XLA Ops:
  0.6 42.2 %shard_map.41 = f32[2,2,3,16,8,128]{5,4,3,2,1,0:T(8,128)S(1)} custom-call(f32[2,3,16,8,128]{4,3,2,1,0:T(8,128)} %orb_hbm.1, f32[16,8,128]{2,1,0:T(8,128)} %pot_hbm.1), custom_call_target="tpu_custom_call" | custom-call | tf_op jit(solution)/shard_map/pallas_call | solution.py:481
  42.9 0.9 %slice_bitcast_fusion = (f32[2,3,16,8,128]{4,3,2,1,0:T(8,128)}, f32[2,3,16,8,128]{4,3,2,1,0:T(8,128)}) fusion(f32[2,2,3,16,8,128]{5,4,3,2,1,0:T(8,128)S(1)} %shard_map.41), kind=kLoop, calls=%fused_computation | loop fusion | bytes 1572864 | tf_op jit(solution)/shard_map/squeeze | solution.py:515

commit v8 on v6

--- a/solution.py
+++ b/solution.py
@@ -116,7 +116,7 @@
 ):
     (ux, *us) = scratch[:NB + 2 - NB // GROUP]
     us = [ux.at[k // GROUP] if k % GROUP == 0 and k < NB else us.pop(0) for k in range(NB + 1)]
-    (stage, pot, ballast, pr, pi, qf, weight, gram, part_y, part_x,
+    (pot, ballast, pr, pi, qf, weight, gram, part_y, part_x,
      ready, load_sem, pot_sem, send_sem, recv_sem, ysend_sem, yrecv_sem, xsend_sem, xrecv_sem) = scratch[NB + 2 - NB // GROUP:]
     norb, bx = orb_hbm.shape[1], orb_hbm.shape[2]
     io, ix, iy = lax.axis_index("orb"), lax.axis_index("gx"), lax.axis_index("gyz")
@@ -124,8 +124,11 @@
 
     load_pot = pltpu.make_async_copy(pot_hbm, pot.at[pl.ds(NEAR, bx), rows], load_sem.at[0])
     load_pot.start()
-    load_orb = pltpu.make_async_copy(orb_hbm, stage, load_sem.at[1])
-    load_orb.start()
+    for o in range(norb):
+        for c in range(2):
+            pltpu.make_async_copy(
+                orb_hbm.at[c, o], us[0].at[o, pl.ds(WIDTH, bx), c, rows], load_sem.at[1 + o]
+            ).start()
 
     low_x, high_x, low_y, high_y = ix > 0, ix < nx - 1, iy > 0, iy < ny - 1
     exists = {-1: (low_x, low_y), 0: (None, None), 1: (high_x, high_y)}
@@ -254,19 +257,15 @@
     gram[...] = jnp.zeros_like(gram)
 
     load_pot.wait()
-    load_orb.wait()
-
-    def unpack(o):
-        for x in range(bx):
-            for c in range(2):
-                us[0][o, x + WIDTH, c, rows] = stage[c, o, x]
-
-    unpack(0)
+
+    def loaded(o):
+        block = us[0].at[o, pl.ds(WIDTH, bx), :, rows]
+        pltpu.make_async_copy(block, block, load_sem.at[1 + o]).wait()
+
     await_greetings(barrier, first)
     each_side(lambda side: pot_halo(side).start())
-    send(0, 0)
-    for o in range(1, norb):
-        unpack(o)
+    for o in range(norb):
+        loaded(o)
         send(0, o)
     greet(ready.at[0], rounds[0])
 
@@ -462,7 +461,7 @@
             out_ref[1, 0, o, x] = re - q * im
             out_ref[1, 1, o, x] = im + q * re
             for c in range(2):
-                out_ref[0, c, o, x] = stage[c, o, x] + inc[c]
+                out_ref[0, c, o, x] = us[0][o, x + WIDTH, c, rows] + inc[c]
             return carry
 
         lax.fori_loop(0, bx, combine, 0, unroll=4)
@@ -487,7 +486,6 @@
             ] + [
                 pltpu.VMEM((norb, bx + 2 * WIDTH, 2, by + 16, nz), jnp.float32) for _ in range(NB + 1 - NB // GROUP)
             ] + [
-                pltpu.VMEM(orbitals.shape, jnp.float32),
                 pltpu.VMEM((bx + 2 * NEAR, by + 16, nz), jnp.float32),
                 pltpu.VMEM((4 * (WIDTH * 8 + bx * WIDTH + 2 * NEAR * NEAR), nz), jnp.float32),
                 pltpu.VMEM((bx + 2 * NEAR, 16, nz), jnp.float32),
@@ -498,7 +496,7 @@
                 pltpu.VMEM((norb, ny, 1, 128), jnp.float32),
                 pltpu.VMEM((norb, nx, 1, 128), jnp.float32),
                 pltpu.SemaphoreType.REGULAR((NB // GROUP,)),
-                pltpu.SemaphoreType.DMA((2,)),
+                pltpu.SemaphoreType.DMA((1 + norb,)),
                 pltpu.SemaphoreType.DMA((2,)),
                 pltpu.SemaphoreType.DMA((8,)),
                 pltpu.SemaphoreType.DMA((2, norb)),

time: 43.7 us -> 43.8 us (level)
  no operation moved by 1% of the time
where the time goes in v8:
time: 43.8 us; the launch traced here: 43.6 us
  Pallas kernels  42.1 us (96%)
  local copies, waits for them, and re-layouts  0.93 us (2%)
  between operations  0.64 us (1%)
    pallas_call x1, Pallas kernels, shards(): pl.pallas_call(functools.partial(kernel, nx, ny), out_shape=jax.ShapeDtyp...  42.1 us
    squeeze x1, local copies, waits for them, and re-layouts, shards(): return (both[0], both[1])  0.93 us

profile of v8, /device:TPU:6, one launch (start us, length us, event | category | flops | bytes accessed | tf_op | source)
XLA Modules:
  0.0 43.6 jit_solution(8519048339151437617)
XLA Ops:
  0.6 42.1 %shard_map.41 = f32[2,2,3,16,8,128]{5,4,3,2,1,0:T(8,128)S(1)} custom-call(f32[2,3,16,8,128]{4,3,2,1,0:T(8,128)} %orb_hbm.1, f32[16,8,128]{2,1,0:T(8,128)} %pot_hbm.1), custom_call_target="tpu_custom_call" | custom-call | tf_op jit(solution)/shard_map/pallas_call | solution.py:479
  42.7 0.9 %slice_bitcast_fusion = (f32[2,3,16,8,128]{4,3,2,1,0:T(8,128)}, f32[2,3,16,8,128]{4,3,2,1,0:T(8,128)}) fusion(f32[2,2,3,16,8,128]{5,4,3,2,1,0:T(8,128)S(1)} %shard_map.41), kind=kLoop, calls=%fused_computation | loop fusion | bytes 1572864 | tf_op jit(solution)/shard_map/squeeze | solution.py:512
